TPU v7x, 32 devices: a whole 2x2x4 slice. The times are simulated.
32 devices in a mesh: wide: 16 (over z, y, x), narrow: 2 (over core).
Axes of the slice: x: 2, y: 2, z: 4, core: 2. Of those that a mesh axis runs over, the one named last changes fastest.
Arguments:
- features: bfloat16 [512, 16384], P('wide', 'narrow'), may hold values from -6 to 6
- queries: bfloat16 [1024, 16384], P('wide', 'narrow'), may hold values from -6 to 6
- damping: float32 [16384], P('wide'), may hold values from 0.25 to 4
Outputs:
- kernel: float32 [16384, 16384], P('wide', 'narrow')
- factor: float32 [16384, 256], P('wide')
- scores: float32 [1024, 512], P('wide', 'narrow')
All inputs are finite; a program needn't handle non-finite values.
Results may differ from a plain program's by a relative error of at most 0.0003.
Values may be sent and summed in bfloat16 or wider, within the bound.
No kernel may reach another device: no remote copies, remote signals or barrier semaphores. Data moves between devices by JAX's collectives and lax.ppermute only.
A program may use at most 128 MiB of HBM per device.

v0:
```python
import math

import jax
import jax.numpy as jnp
from jax import lax
from jax.sharding import PartitionSpec as P

P_SIZE = 16384
PANEL = 128
PANELS = 2


def broadcast(x, axis, root):
    mine = lax.axis_index(axis) == root
    return lax.psum(jnp.where(mine, x, jnp.zeros_like(x)), axis)


def on_device(features, queries, damping):
    rows_here = damping.shape[0]
    cols_here = queries.shape[1]
    slab_total = features.shape[0] * lax.axis_size("wide")
    wide_pos = lax.axis_index("wide")
    narrow_pos = lax.axis_index("narrow")
    contract_rows = (((0,), (0,)), ((), ()))
    contract_cols = (((1,), (1,)), ((), ()))
    full_width = lax.all_gather(features, "narrow", axis=1, tiled=True)
    row_features = lax.all_to_all(full_width, "wide", split_axis=1, concat_axis=0, tiled=True)
    slab_columns = lax.all_gather(features, "wide", axis=0, tiled=True)
    products = lax.dot_general(
        row_features, slab_columns, contract_rows, preferred_element_type=jnp.float32
    )
    partial_value = lax.dot_general(
        queries, slab_columns, contract_cols, preferred_element_type=jnp.float32
    )
    scores = lax.psum_scatter(partial_value, "narrow", scatter_dimension=1, tiled=True) * (
        1.0 / math.sqrt(P_SIZE)
    )
    row_ids = wide_pos * rows_here + lax.broadcasted_iota(jnp.int32, (rows_here, 1), 0)
    col_ids = narrow_pos * cols_here + lax.broadcasted_iota(jnp.int32, (1, cols_here), 1)
    kernel_block = products / slab_total + jnp.where(
        row_ids == col_ids, damping[:, None], jnp.float32(0.0)
    )
    factors = []
    for panel_index in range(PANELS):
        offset = panel_index * PANEL
        column_root = offset // cols_here
        row_root = offset // rows_here
        col_shift = offset % cols_here
        row_shift = offset % rows_here
        panel_columns = broadcast(
            kernel_block[:, col_shift : col_shift + PANEL], "narrow", column_root
        )
        pivot_block = broadcast(panel_columns[row_shift : row_shift + PANEL], "wide", row_root)
        pivot_factor = jnp.linalg.cholesky(pivot_block)
        lower_rows = lax.linalg.triangular_solve(
            pivot_factor, panel_columns, left_side=False, lower=True, transpose_a=True
        )
        pivot_rows = broadcast(kernel_block[row_shift : row_shift + PANEL], "wide", row_root)
        lower_cols = lax.linalg.triangular_solve(
            pivot_factor, pivot_rows, left_side=True, lower=True, transpose_a=False
        ).T
        kernel_block = kernel_block - jnp.dot(
            lower_rows,
            lower_cols.T,
            precision=lax.Precision.HIGHEST,
            preferred_element_type=jnp.float32,
        )
        boundary = offset + PANEL
        kernel_block = jnp.where(
            (row_ids < boundary) | (col_ids < boundary), jnp.zeros_like(kernel_block), kernel_block
        )
        factors.append(lower_rows)
    return (kernel_block, jnp.concatenate(factors, axis=1), scores)


def solution(mesh):
    return jax.shard_map(
        on_device,
        mesh=mesh,
        in_specs=(P("wide", "narrow"), P("wide", "narrow"), P("wide")),
        out_specs=(P("wide", "narrow"), P("wide", None), P("wide", "narrow")),
        check_vma=False,
    )
```

profile of v0, /device:TPU:0, one launch (start us, length us, event | category | flops | bytes accessed | tf_op | source)
XLA Modules:
  0.0 752.9 jit_solution(7625984602944274443)
XLA Ops:
  8.7 12.7 %all-gather.3.cloned.1.call-done = bf16[32,16384]{1,0:T(8,128)(2,1)} async-done(((bf16[32,8192]{1,0:T(8,128)(2,1)}), bf16[32,16384]{1,0:T(8,128)(2,1)}) %all-gather.3.cloned.1.call-update) | async-done | bytes 1048592 | tf_op jit(solution)/shard_map/all_gather | solution.py:26
  21.3 2.3 copy.41
  23.6 6.8 all-to-all-start
  30.5 35.8 %all-to-all-done = bf16[32,16,1024]{2,0,1:T(8,128)(2,1)S(1)} async-done(((bf16[32,16,1024]{2,0,1:T(8,128)(2,1)}), bf16[32,16,1024]{2,0,1:T(8,128)(2,1)S(1)}, u32[]{:S(2)}, u32[]{:S(2)}) %all-to-all-start) | async-done | bytes 1048608 | tf_op jit(solution)/shard_map/all_to_all | solution.py:27
  66.3 85.7 %all-gather.5.cloned.1.call-done = bf16[512,8192]{1,0:T(8,128)(2,1)} async-done(((bf16[32,8192]{1,0:T(8,128)(2,1)}), bf16[512,8192]{1,0:T(8,128)(2,1)}) %all-gather.5.cloned.1.call-update) | async-done | bytes 8388624 | tf_op jit(solution)/shard_map/all_gather | solution.py:28
  151.9 19.3 %select_add_fusion = f32[1024,8192]{0,1:T(8,128)} fusion(bf16[512,1024]{1,0:T(8,128)(2,1)S(1)} %bitcast.49, bf16[512,8192]{1,0:T(8,128)(2,1)} %all-gather.5.cloned.1.call-done, f32[1024]{0:T(1024)} %param.10, s32[1024]{0:T(1024)S(1)} %iota_add_fusion.1, s32[8192]{0:T(1024)S(1)} %iota_add_fusion), kind=kOutput, calls=%fused_computation.2 | convolution fusion | flops 8623489024 | bytes 43032576 | tf_op jit(solution)/shard_map/dot_general | solution.py:29
  171.3 1.9 slice_select_fusion.3
  173.2 4.4 slice_select_fusion.1
  177.6 12.5 %all-reduce.7.cloned.1.call-done = f32[1024,128]{0,1:T(8,128)} async-done(((f32[1024,128]{0,1:T(8,128)}), f32[1024,128]{0,1:T(8,128)}) %all-reduce.7.cloned.1.call-update) | async-done | bytes 524304 | tf_op jit(solution)/shard_map/psum | solution.py:15
  190.1 1.5 slice_select_fusion.5
  192.1 175.9 %all-reduce.13.cloned.1.call-done = (f32[128,128]{0,1:T(8,128)}, f32[128,8192]{0,1:T(8,128)}) async-done(((f32[128,128]{0,1:T(8,128)}, f32[128,8192]{0,1:T(8,128)}), (f32[128,128]{0,1:T(8,128)}, f32[128,8192]{0,1:T(8,128)})) %all-reduce.13.cloned.1.call-update) | async-done | bytes 4259856 | tf_op jit(solution)/shard_map/psum | solution.py:15
  368.0 0.9 copy.30
  368.9 0.9 fusion.9
  369.7 11.7 %cholesky.44 = f32[128,128]{1,0:T(8,128)S(1)} custom-call(f32[128,128]{1,0:T(8,128)S(1)} %fusion.9), custom_call_target="Cholesky" | custom-call | tf_op jit(solution)/shard_map/jit(cholesky)/cholesky | solution.py:54
  382.8 9.8 %custom-call.10 = f32[1,128,128]{1,2,0:T(8,128)S(1)} custom-call(f32[1,128,128]{2,1,0:T(8,128)S(1)} %fusion), custom_call_target="InvertDiagBlocksLowerTriangular" | custom-call | tf_op jit(solution)/shard_map/triangular_solve/custom-call.0 | solution.py:55
  392.6 6.1 fusion.6
  399.3 35.1 %subtract_select_fusion.1 = f32[1024,8192]{0,1:T(8,128)} fusion(f32[1024,8192]{0,1:T(8,128)} %select_add_fusion, f32[1024,128]{0,1:T(8,128)S(1)} %convolution_bitcast_fusion.1, f32[128,8192]{1,0:T(8,128)S(1)} %fusion.6, pred[1024]{0:T(1024)(128)(4,1)S(1)} %fusion.12, pred[8192]{0:T(1024)(128)(4,1)S(1)} %fusion.10), kind=kOutput, calls=%fused_computation.1 | convolution fusion | flops 12910067712 | bytes 71836672 | tf_op jit(solution)/shard_map/dot_general | solution.py:62
  434.5 1.9 slice_select_fusion.2
  436.4 6.7 fusion.14
  443.4 4.4 slice_select_fusion
  447.8 6.4 all-reduce.9.cloned.1.call-done
  454.2 1.5 slice_select_fusion.4
  455.8 9.3 %reduce-scatter.2.cloned.1.call-done = f32[64,256]{1,0:T(8,128)} async-done(((f32[64,512]{1,0:T(8,128)}), f32[64,256]{1,0:T(8,128)}) %reduce-scatter.2.cloned.1.call-update) | async-done | bytes 65552 | tf_op jit(solution)/shard_map/reduce_scatter | solution.py:35
  465.1 1.5 broadcast_multiply_fusion
  466.5 176.4 %all-reduce.11.cloned.1.call-done = (f32[128,128]{0,1:T(8,128)}, f32[128,8192]{0,1:T(8,128)}) async-done(((f32[128,128]{0,1:T(8,128)}, f32[128,8192]{0,1:T(8,128)}), (f32[128,128]{0,1:T(8,128)}, f32[128,8192]{0,1:T(8,128)})) %all-reduce.11.cloned.1.call-update) | async-done | bytes 4259856 | tf_op jit(solution)/shard_map/psum | solution.py:15
  643.0 0.9 copy.32
  644.7 11.7 %cholesky.55 = f32[128,128]{1,0:T(8,128)S(1)} custom-call(f32[128,128]{1,0:T(8,128)S(1)} %fusion.5), custom_call_target="Cholesky" | custom-call | tf_op jit(solution)/shard_map/jit(cholesky)/cholesky | solution.py:54
  657.8 9.8 %custom-call.12 = f32[1,128,128]{1,2,0:T(8,128)S(1)} custom-call(f32[1,128,128]{2,1,0:T(8,128)S(1)} %fusion.1), custom_call_target="InvertDiagBlocksLowerTriangular" | custom-call | tf_op jit(solution)/shard_map/triangular_solve/custom-call.0 | solution.py:55
  667.6 8.0 %fusion.2 = f32[128,8192]{1,0:T(8,128)} fusion(f32[128,8192]{0,1:T(8,128)} %get-tuple-element.19, f32[1,128,128]{1,2,0:T(8,128)S(1)} %custom-call.12), kind=kOutput, calls=%fused_computation.17 | convolution fusion | flops 1610612736 | bytes 8454144 | tf_op jit(solution)/shard_map/triangular_solve/dot.0 | solution.py:59
  676.3 1.3 copy.35
  677.7 37.0 %subtract_select_fusion = f32[1024,8192]{0,1:T(8,128)} fusion(f32[1024,8192]{0,1:T(8,128)} %subtract_select_fusion.1, f32[1024,128]{0,1:T(8,128)S(1)} %convolution_bitcast_fusion, f32[128,8192]{1,0:T(8,128)} %fusion.2, pred[1024]{0:T(1024)(128)(4,1)S(1)} %fusion.13, pred[8192]{0:T(1024)(128)(4,1)S(1)} %fusion.11), kind=kOutput, calls=%fused_computation | convolution fusion | flops 12910067712 | bytes 71836672 | tf_op jit(solution)/shard_map/dot_general | solution.py:62
  714.6 31.2 %copy.34 = f32[1024,8192]{1,0:T(8,128)} copy(f32[1024,8192]{0,1:T(8,128)} %subtract_select_fusion) | data formatting | bytes 67108864
  (38 shorter events, 7.1 us)
Async XLA Ops:
  7.2 429.3 %copy-start = (bf16[64,8192]{1,0:T(8,128)(2,1)S(1)}, bf16[64,8192]{1,0:T(8,128)(2,1)}, u32[]{:S(2)}) copy-start(bf16[64,8192]{1,0:T(8,128)(2,1)} %param.9) | copy-start | bytes 3145732
  7.2 14.1 %all-gather.3.cloned.1.call-start = ((), (), s32[]{:S(2)}) async-start(), calls=%async_computation.2 | async-start | bytes 1572864 | tf_op jit(solution)/shard_map/all_gather | solution.py:26
  7.9 144.0 %all-gather.5.cloned.1.call-start = ((), (), s32[]{:S(2)}) async-start(), calls=%async_computation.3 | async-start | bytes 8912896 | tf_op jit(solution)/shard_map/all_gather | solution.py:28
  23.6 42.7 %all-to-all-start = ((bf16[32,16,1024]{2,0,1:T(8,128)(2,1)}), bf16[32,16,1024]{2,0,1:T(8,128)(2,1)S(1)}, u32[]{:S(2)}, u32[]{:S(2)}) async-start(bf16[32,16,1024]{2,0,1:T(8,128)(2,1)} %bitcast.48), calls=%async_computation | async-start | bytes 2097152 | tf_op jit(solution)/shard_map/all_to_all | solution.py:27
  30.4 159.7 %all-reduce.7.cloned.1.call-start = ((), (), s32[]{:S(2)}) async-start(), calls=%async_computation.4 | async-start | bytes 1048576 | tf_op jit(solution)/shard_map/psum | solution.py:15
  173.2 194.8 %all-reduce.13.cloned.1.call-start = ((), (), s32[]{:S(2)}) async-start(), calls=%async_computation.8 | async-start | bytes 8519680 | tf_op jit(solution)/shard_map/psum | solution.py:15
  190.1 208.6 %copy-start.3 = (f32[1024,128]{0,1:T(8,128)S(1)}, f32[1024,128]{0,1:T(8,128)}, u32[]{:S(2)}) copy-start(f32[1024,128]{0,1:T(8,128)} %all-reduce.7.cloned.1.call-done) | copy-start | bytes 1572868
  191.7 262.5 %all-reduce.9.cloned.1.call-start = ((), (), s32[]{:S(2)}) async-start(), calls=%async_computation.5 | async-start | bytes 1048576 | tf_op jit(solution)/shard_map/psum | solution.py:15
  436.4 28.7 %reduce-scatter.2.cloned.1.call-start = ((), (), s32[]{:S(2)}) async-start(), calls=%async_computation.6 | async-start | bytes 196608 | tf_op jit(solution)/shard_map/reduce_scatter | solution.py:35
  443.2 199.8 %all-reduce.11.cloned.1.call-start = ((), (), s32[]{:S(2)}) async-start(), calls=%async_computation.7 | async-start | bytes 8519680 | tf_op jit(solution)/shard_map/psum | solution.py:15
  454.2 221.4 %copy-start.2 = (f32[1024,128]{0,1:T(8,128)S(1)}, f32[1024,128]{0,1:T(8,128)}, u32[]{:S(2)}) copy-start(f32[1024,128]{0,1:T(8,128)} %all-reduce.9.cloned.1.call-done) | copy-start | bytes 1572868
  714.6 31.2 %copy-start.1 = (bf16[64,8192]{1,0:T(8,128)(2,1)S(1)}, bf16[64,8192]{1,0:T(8,128)(2,1)}, u32[]{:S(2)}) copy-start(bf16[64,8192]{1,0:T(8,128)(2,1)} %param.9) | copy-start | bytes 3145732
Sparse Core Ops, SparseCore 0:
  9.5 11.7 all-gather.2
  24.1 127.8 all-gather.4
  173.3 16.7 all-reduce.6
  196.5 171.4 all-reduce.12
  436.5 17.6 all-reduce.8
  456.2 8.7 reduce-scatter.1
  471.6 171.3 all-reduce.10
where the time goes:
time: 759 us; the launch traced here: 753 us
  waiting for transfers between devices  516 us (68%)
  matrix products  113 us (15%)
  other arithmetic  64.7 us (9%)
  local copies, waits for them, and re-layouts  36.6 us (5%)
  between operations  14.5 us (2%)
    psum x4, waiting for transfers between devices, broadcast(): return lax.psum(jnp.where(mine, x, jnp.zeros_like(x)), axis)  371 us
    all_gather x1, waiting for transfers between devices, on_device(): slab_columns = lax.all_gather(features, 'wide', axis=0, tiled=True)  85.7 us
    dot_general x2, matrix products, on_device(): jnp.dot(lower_rows, lower_cols.T, precision=lax.Precision.HIGHEST, prefer...  72.1 us
    all_to_all x1, waiting for transfers between devices, on_device(): lax.all_to_all(full_width, 'wide', split_axis=1, concat_axis=0, tiled=True)  35.8 us
    unnamed x10, local copies, waits for them, and re-layouts  32.5 us
    another operation x6, other arithmetic, on_device(): pivot_factor = jnp.linalg.cholesky(pivot_block)  24.8 us
    another operation x4, other arithmetic, on_device(): lax.linalg.triangular_solve(pivot_factor, panel_columns, left_side=False,...  20.9 us
    dot_general x1, matrix products, on_device(): lax.dot_general(row_features, slab_columns, contract_rows, preferred_elem...  19.3 us
  transfers between devices with their start and end apart: 8, of which 8 were waited for; matrix products, arithmetic and copies ran while one was open for 3% of the time, Pallas kernels for 0%

commit v1 on v0

v1 whole, which is shorter than its diff:
```python
import math

import jax
import jax.numpy as jnp
from jax import lax
from jax.experimental import pallas as pl
from jax.experimental.pallas import tpu as pltpu
from jax.sharding import PartitionSpec as P


PANEL = 128
PANELS = 2
PIVOTS = PANEL * PANELS
TILE = 512
SLOTS = 4
HIGHEST = lax.Precision.HIGHEST


def dot(a, b, ca, cb, precision=None):
    return lax.dot_general(
        a, b, (((ca,), (cb,)), ((), ())), precision=precision, preferred_element_type=jnp.float32
    )


def split_bf16(value, parts):
    pieces = []
    for _ in range(parts):
        piece = lax.reduce_precision(value, 8, 7)
        pieces.append(piece.astype(jnp.bfloat16))
        value = value - piece
    return pieces


def inverse_factor(block, a_s, w_s):
    n = block.shape[0]
    sub = lax.broadcasted_iota(jnp.int32, (n, n), 0)
    lane = lax.broadcasted_iota(jnp.int32, (n, n), 1)
    lane8 = lax.broadcasted_iota(jnp.int32, (8, n), 1)
    sub8 = lax.broadcasted_iota(jnp.int32, (8, 1), 0)
    sub_col = lax.broadcasted_iota(jnp.int32, (n, 1), 0)
    a_s[...] = block
    w_s[...] = jnp.where(sub == lane, 1.0, 0.0)

    def step(b, carry):
        k0 = pl.multiple_of(b * 8, 8)
        rows = a_s[pl.ds(k0, 8), :]
        wrows = w_s[pl.ds(k0, 8), :]
        a = a_s[...]
        heads = [jnp.sum(jnp.where(lane8 == k0 + j, rows, 0.0), axis=1, keepdims=True) for j in range(8)]
        columns = [jnp.sum(jnp.where(lane == k0 + j, a, 0.0), axis=1, keepdims=True) for j in range(8)]
        scaled = []
        for j in range(8):
            inv = 1.0 / heads[j][j : j + 1, :]
            times = jnp.where(sub8 > j, heads[j], 0.0) * inv
            for m in range(j + 1, 8):
                entry = heads[m][j : j + 1, :]
                columns[m] = columns[m] - columns[j] * (entry * inv)
                heads[m] = heads[m] - times * entry
            scaled.append((rows[j : j + 1, :] * inv, wrows[j : j + 1, :] * inv))
            rows = rows - times * rows[j : j + 1, :]
            wrows = wrows - times * wrows[j : j + 1, :]
        w = w_s[...]
        for j in range(8):
            column = jnp.where(sub_col > k0 + 7, columns[j], 0.0)
            a = a - column * scaled[j][0]
            w = w - column * scaled[j][1]
        a_s[...] = a
        w_s[...] = w
        a_s[pl.ds(k0, 8), :] = rows
        w_s[pl.ds(k0, 8), :] = wrows
        return carry

    lax.fori_loop(0, n // 8, step, 0)
    diagonal = jnp.sum(jnp.where(sub == lane, a_s[...], 0.0), axis=1, keepdims=True)
    return w_s[...] * (1.0 / jnp.sqrt(diagonal))


def first_panel_body(slab, each, place_ref, packed_ref, other_ref, fp_ref, inv_ref, left_ref, rest_ref, a_s, w_s):
    mine = place_ref[1] == 0
    fp = jnp.where(mine, packed_ref[:, :each, :], other_ref[:, :each, :]).reshape(slab, PIVOTS)
    fp_ref[...] = fp
    tail = pl.ds(each, 16)
    tail = jnp.where(mine, packed_ref[place_ref[0], tail, :], other_ref[place_ref[0], tail, :])
    tail = tail.astype(jnp.float32)
    damping = tail[0:1, :] + tail[1:2, :] + tail[2:3, :]
    sub = lax.broadcasted_iota(jnp.int32, (PIVOTS, PIVOTS), 0)
    lane = lax.broadcasted_iota(jnp.int32, (PIVOTS, PIVOTS), 1)
    pivots = dot(fp, fp, 0, 0) / slab + jnp.where(sub == lane, damping, 0.0)
    inv = inverse_factor(pivots[:PANEL, :PANEL], a_s, w_s)
    left = dot(pivots[PANEL:, :PANEL], inv, 1, 1, HIGHEST)
    inv_ref[...] = inv
    left_ref[...] = left
    rest_ref[...] = pivots[PANEL:, PANEL:] - dot(left, left, 1, 1, HIGHEST)


def first_panel(place, packed, other, slab, each):
    f32 = jax.ShapeDtypeStruct((PANEL, PANEL), jnp.float32)
    return pl.pallas_call(
        lambda *refs: first_panel_body(slab, each, *refs),
        in_specs=[pl.BlockSpec(memory_space=pltpu.SMEM), pl.BlockSpec(memory_space=pltpu.VMEM)]
        + [pl.BlockSpec(memory_space=pltpu.VMEM)],
        out_shape=(jax.ShapeDtypeStruct((slab, PIVOTS), jnp.bfloat16), f32, f32, f32),
        scratch_shapes=[pltpu.VMEM((PANEL, PANEL), jnp.float32)] * 2,
        name="first_panel",
    )(place, packed, other)


def second_panel_body(inv_ref, left_ref, rest_ref, fp_ref, full_ref, middle_ref, a_s, w_s):
    slab = fp_ref.shape[0]
    first = inv_ref[...]
    inv = inverse_factor(rest_ref[...], a_s, w_s)
    below = -dot(dot(inv, left_ref[...], 1, 0, HIGHEST), first, 1, 0, HIGHEST)
    top = jnp.concatenate([first, jnp.zeros((PANEL, PANEL), jnp.float32)], axis=1)
    full = jnp.concatenate([top, jnp.concatenate([below, inv], axis=1)], axis=0)
    full_ref[...] = full
    basis = dot(full, fp_ref[...].astype(jnp.float32), 1, 1, HIGHEST)
    sub = lax.broadcasted_iota(jnp.int32, (slab, slab), 0)
    lane = lax.broadcasted_iota(jnp.int32, (slab, slab), 1)
    middle = jnp.where(sub == lane, 1.0, 0.0) - dot(basis, basis, 0, 0, HIGHEST) / slab
    for part in range(3):
        piece = middle.astype(jnp.bfloat16)
        middle_ref[part] = piece
        middle = middle - piece.astype(jnp.float32)


def second_panel(inv, left, rest, fp):
    slab = fp.shape[0]
    parts = jax.ShapeDtypeStruct((3, slab, slab), jnp.bfloat16)
    return pl.pallas_call(
        second_panel_body,
        out_shape=(jax.ShapeDtypeStruct((PIVOTS, PIVOTS), jnp.float32), parts),
        scratch_shapes=[pltpu.VMEM((PANEL, PANEL), jnp.float32)] * 2,
        name="second_panel",
    )(inv, left, rest, fp)


def group_scan_body(home_ref, queries_ref, own_ref, x_ref, y_ref, a_ref, b_ref, partial_ref, rows_ref):
    rows_here = rows_ref.shape[1]
    halves = a_ref.shape[1] // rows_here
    columns = [own_ref[...], x_ref[...], y_ref[...], jnp.concatenate([a_ref[...], b_ref[...]], axis=1)]
    partial_ref[...] = dot(jnp.concatenate(columns, axis=0), queries_ref[...], 1, 1)
    home = home_ref[0]
    at = pl.ds(pl.multiple_of(home * rows_here, 128), rows_here)
    early = pl.ds(pl.multiple_of(jnp.minimum(home, halves - 1) * rows_here, 128), rows_here)
    late = pl.ds(pl.multiple_of(jnp.maximum(home - halves, 0) * rows_here, 128), rows_here)
    diag = jnp.where(home < halves, a_ref[:, early], b_ref[:, late])
    rows_ref[...] = jnp.concatenate([own_ref[:, at], x_ref[:, at], y_ref[:, at], diag], axis=0)


def group_scan(home, queries, group, rows_here):
    each = group[0].shape[0]
    return pl.pallas_call(
        group_scan_body,
        in_specs=[pl.BlockSpec(memory_space=pltpu.SMEM)] + [pl.BlockSpec(memory_space=pltpu.VMEM)] * 6,
        out_shape=(
            jax.ShapeDtypeStruct((4 * each, queries.shape[0]), jnp.float32),
            jax.ShapeDtypeStruct((4 * each, rows_here), jnp.bfloat16),
        ),
        name="group_scan",
    )(home, queries, *group)


def row_sums(home, refs, at, fp_ref, middle_ref):
    rows = [jnp.where(home == 1, mine[...], other[...]) for mine, other in zip(*[iter(refs)] * 2)]
    rows = jnp.concatenate(rows, axis=0).T
    middle = jnp.concatenate([middle_ref[part, k] for part in range(3) for k in at], axis=0)
    front = jnp.concatenate([fp_ref[k] for k in at], axis=0)
    return dot(jnp.concatenate([rows] * 3, axis=1), middle, 1, 0), dot(rows, front, 1, 0)


def early_rows(home, groups, fp, middle, row_parts):
    size, rows_here = row_parts[0].shape
    slab = fp.shape[0]

    def body(home_ref, fp_ref, middle_ref, *refs):
        left, ahead = row_sums(home_ref[1], refs[:-2], groups, fp_ref, middle_ref)
        refs[-2][...] = left
        refs[-1][...] = ahead

    return pl.pallas_call(
        body,
        in_specs=[pl.BlockSpec(memory_space=pltpu.SMEM)]
        + [pl.BlockSpec(memory_space=pltpu.VMEM)] * (2 + len(row_parts)),
        out_shape=(
            jax.ShapeDtypeStruct((rows_here, slab), jnp.float32),
            jax.ShapeDtypeStruct((rows_here, PIVOTS), jnp.float32),
        ),
        name="early_rows",
    )(home, fp.reshape(-1, size, PIVOTS), middle.reshape(3, -1, size, slab), *row_parts)


def kernel_block_body(
    last, tile, ids_ref, damp_ref, early_ref, ahead_ref, fp_ref, inv_ref, middle_ref, mine_ref, other_ref, *refs
):
    out_ref, factor_ref, hi_s, lo_s, factor_s, slots, sems, factor_sem = refs[-8:]
    groups = list(zip(*[iter(refs[:-8])] * 5))
    rows, slab = hi_s.shape
    steps = out_ref.shape[1] // tile
    half_steps = steps // 2
    row0 = ids_ref[0]
    left, ahead = row_sums(ids_ref[2], [mine_ref, other_ref], [last], fp_ref, middle_ref)
    left = (left + early_ref[...]) / slab
    hi = left.astype(jnp.bfloat16)
    hi_s[...] = hi
    lo_s[...] = (left - hi.astype(jnp.float32)).astype(jnp.bfloat16)
    row_ids = row0 + lax.broadcasted_iota(jnp.int32, (rows, PIVOTS), 0)
    pivot_ids = lax.broadcasted_iota(jnp.int32, (rows, PIVOTS), 1)
    ahead = (ahead + ahead_ref[...]) / slab
    ahead = ahead + jnp.where(row_ids == pivot_ids, damp_ref[:, :PIVOTS], 0.0)
    factor_s[...] = dot(ahead, inv_ref[...], 1, 1, HIGHEST)
    factor_copy = pltpu.make_async_copy(factor_s, factor_ref, factor_sem)
    factor_copy.start()

    def store(step, slot):
        at = pl.ds(pl.multiple_of(step * tile, 128), tile)
        return pltpu.make_async_copy(slots.at[slot], out_ref.at[:, at], sems.at[slot])

    def one(step, carry):
        slot = lax.rem(step, SLOTS)
        col0 = ids_ref[1] + step * tile
        at = pl.ds(pl.multiple_of(step * tile, 128), tile)
        early = pl.ds(pl.multiple_of(jnp.minimum(step, half_steps - 1) * tile, 128), tile)
        late = pl.ds(pl.multiple_of(jnp.maximum(step - half_steps, 0) * tile, 128), tile)
        pieces = []
        for own, across_x, across_y, diag_a, diag_b in groups:
            diag = jnp.where(step < half_steps, diag_a[:, early], diag_b[:, late])
            pieces += [own[:, at], across_x[:, at], across_y[:, at], diag]
        columns = jnp.concatenate(pieces, axis=0)

        @pl.when(step >= SLOTS)
        def _():
            store(step - SLOTS, slot).wait()

        slots[slot] = dot(hi_s[...], columns, 1, 0) + dot(lo_s[...], columns, 1, 0)

        @pl.when((col0 < row0 + rows) & (row0 < col0 + tile))
        def _():
            row_ids = row0 + lax.broadcasted_iota(jnp.int32, (rows, tile), 0)
            col_ids = col0 + lax.broadcasted_iota(jnp.int32, (rows, tile), 1)
            own_at = pl.ds(pl.multiple_of(col0 - row0, 128), tile)
            slots[slot] = slots[slot] + jnp.where(row_ids == col_ids, damp_ref[:, own_at], 0.0)

        @pl.when(row0 < PIVOTS)
        def _():
            slots[slot, :PIVOTS, :] = jnp.zeros((PIVOTS, tile), jnp.float32)

        @pl.when(col0 < PIVOTS)
        def _():
            col_ids = col0 + lax.broadcasted_iota(jnp.int32, (1, tile), 1)
            slots[slot] = jnp.where(col_ids < PIVOTS, 0.0, slots[slot])

        store(step, slot).start()
        return carry

    lax.fori_loop(0, steps, one, 0)
    for step in range(max(0, steps - SLOTS), steps):
        store(step, step % SLOTS).wait()
    factor_copy.wait()


def kernel_block(ids, damping, early, fp, inverses, middle, last, rows_last, pieces):
    cols_here = pieces[0][0].shape[1]
    size, rows = rows_last[0].shape
    slab = fp.shape[0]
    tile = min(TILE, rows, cols_here // 2)
    fixed = [damping, *early, fp.reshape(-1, size, PIVOTS), inverses, middle.reshape(3, -1, size, slab), *rows_last]
    fixed += [piece for group in pieces for piece in group]
    return pl.pallas_call(
        lambda *refs: kernel_block_body(last, tile, *refs),
        in_specs=[pl.BlockSpec(memory_space=pltpu.SMEM)]
        + [pl.BlockSpec(memory_space=pltpu.VMEM)] * len(fixed),
        out_specs=(pl.BlockSpec(memory_space=pl.ANY), pl.BlockSpec(memory_space=pl.ANY)),
        out_shape=(
            jax.ShapeDtypeStruct((rows, cols_here), jnp.float32),
            jax.ShapeDtypeStruct((rows, PIVOTS), jnp.float32),
        ),
        scratch_shapes=[
            pltpu.VMEM((rows, slab), jnp.bfloat16),
            pltpu.VMEM((rows, slab), jnp.bfloat16),
            pltpu.VMEM((rows, PIVOTS), jnp.float32),
            pltpu.VMEM((SLOTS, rows, tile), jnp.float32),
            pltpu.SemaphoreType.DMA((SLOTS,)),
            pltpu.SemaphoreType.DMA,
        ],
        cost_estimate=pl.CostEstimate(
            flops=4 * rows * slab * cols_here,
            bytes_accessed=4 * rows * cols_here + 2 * slab * cols_here,
            transcendentals=0,
        ),
        name="kernel_block",
    )(ids, *fixed)


def solution(mesh):
    wide = mesh.shape["wide"]
    narrow = mesh.shape["narrow"]
    depth = wide // 4

    def index(x, y, z):
        return z * 4 + y * 2 + x

    spots = [(x, y, z) for z in range(depth) for y in range(2) for x in range(2)]
    swap_x = [(index(x, y, z), index(1 - x, y, z)) for x, y, z in spots]
    swap_y = [(index(x, y, z), index(x, 1 - y, z)) for x, y, z in spots]

    def shift(s):
        return [(index(x, y, z), index(x, y, (z + s) % depth)) for x, y, z in spots]

    def send(value, moves):
        return lax.ppermute(value, "wide", moves)

    def from_other(value, root):
        if narrow == 2:
            return lax.ppermute(value, "narrow", [(0, 1), (1, 0)])
        mine = lax.axis_index("narrow") == root
        return lax.psum(jnp.where(mine, value, jnp.zeros_like(value)), "narrow")

    sequence = []
    for r in range(1, depth // 2 + 1):
        sequence += [r] if depth - r == r else [r, depth - r]
    last = sequence[-1]

    def on_device(features, queries, damping):
        each, cols_here = features.shape
        rows_here = damping.shape[0]
        slab = each * wide
        half = cols_here // 2
        w = lax.axis_index("wide")
        n = lax.axis_index("narrow")

        damp_parts = jnp.stack(split_bf16(damping[:PIVOTS], 3))
        packed = jnp.concatenate(
            [features[:, :PIVOTS], damp_parts, jnp.zeros((13, PIVOTS), jnp.bfloat16)], axis=0
        )
        packed = jnp.stack([packed, send(packed, swap_x)])
        packed = jnp.concatenate([packed, send(packed, swap_y)], axis=0)
        packed = jnp.stack([packed] + [send(packed, shift(r)) for r in range(1, depth)])
        other = from_other(packed, 0).reshape(wide, each + 16, PIVOTS)
        packed = packed.reshape(wide, each + 16, PIVOTS)
        x, y, z = w % 2, (w // 2) % 2, w // 4
        place = jnp.stack([z * 4 + y * 2 + x, n]).astype(jnp.int32)
        fp, inv, left, rest = first_panel(place, packed, other, slab, each)
        inverses, middle = second_panel(inv, left, rest, fp)

        pieces = [None] * depth
        layers = {0: features}
        for r in [0] + sequence:
            if r and r <= depth // 2:
                layers[r] = send(layers[r - 1], shift(1))
            elif r:
                layers[r] = send(layers[(r + 1) % depth], shift(-1))
            layer = layers[r]
            across_x = send(layer, swap_x)
            across_y = send(layer, swap_y)
            diag_a = send(across_y[:, :half], swap_x)
            diag_b = send(across_x[:, half:], swap_y)
            pieces[r] = (layer, across_x, across_y, diag_a, diag_b)

        home = (w * rows_here) // cols_here
        begin = (w * rows_here) % cols_here // rows_here
        here = jnp.stack([begin, home == n]).astype(jnp.int32)
        row_parts = []
        partial = []
        for r in range(depth):
            part, rows = group_scan(here, queries, pieces[r], rows_here)
            row_parts.append((rows, from_other(rows, home)))
            partial.append(part)
        before = [r for r in range(depth) if r != last]
        early = early_rows(here, before, fp, middle, [rows for r in before for rows in row_parts[r]])

        partial = jnp.concatenate(partial, axis=0)
        spot = lax.broadcasted_iota(jnp.int32, (slab, 1), 0)
        group_id = spot // (4 * each)
        local = (spot // each) % 4
        example = (
            ((z - group_id) % depth) * 4 + (y ^ (local // 2)) * 2 + (x ^ (local % 2))
        ) * each + spot % each
        names = lax.broadcasted_iota(jnp.int32, (1, slab), 1)
        partial = dot(partial, (example == names).astype(jnp.float32), 0, 0, HIGHEST)
        scale = 1.0 / math.sqrt(cols_here * narrow)
        if narrow == 2:
            width = slab // 2
            keep = lax.dynamic_slice_in_dim(partial, n * width, width, axis=1)
            give = lax.dynamic_slice_in_dim(partial, (1 - n) * width, width, axis=1)
            other = lax.ppermute(give, "narrow", [(0, 1), (1, 0)])
            scores = (keep + other) * scale
        else:
            scores = lax.psum_scatter(partial, "narrow", scatter_dimension=1, tiled=True) * scale

        ids = jnp.stack([w * rows_here, n * cols_here, home == n]).astype(jnp.int32)
        kernel, factor = kernel_block(ids, damping[None, :], early, fp, inverses, middle, last, row_parts[last], pieces)
        return kernel, factor, scores

    return jax.shard_map(
        on_device,
        mesh=mesh,
        in_specs=(P("wide", "narrow"), P("wide", "narrow"), P("wide")),
        out_specs=(P("wide", "narrow"), P("wide", None), P("wide", "narrow")),
        check_vma=False,
    )
```

time: 759 us -> 167 us (0.22)
  waiting for transfers between devices: 516 us -> 37.9 us
  matrix products: 113 us -> 1.39 us
  Pallas kernels: 0 us -> 67.4 us
  other arithmetic: 64.7 us -> 4.96 us
  starting transfers between devices: 7.54 us -> 43.6 us
  local copies, waits for them, and re-layouts: 36.6 us -> 10.8 us
  between operations: 14.5 us -> 0.94 us
    psum x4 -> x0, waiting for transfers between devices: 371 us -> none  [broadcast(): return lax.psum(jnp.where(mine, x, jnp.zeros_like(x)), axis)]
    all_gather x2 -> x0, waiting for transfers between devices: 98.3 us -> none  [the longest x1 85.7 us: on_device(): slab_columns = lax.all_gather(features, 'wide', axis=0, tiled=True)]
    dot_general x4 -> x1, matrix products: 98.2 us -> 1.39 us  [dot(): lax.dot_general(a, b, (((ca,), (cb,)), ((), ())), precision=precision, pr...]
    pallas_call x0 -> x8, Pallas kernels: none -> 67.4 us  [the longest x1 31 us: kernel_block(): pl.pallas_call(lambda *refs: kernel_block_body(last, tile, *refs), in_spe...]
    ppermute x0 -> x30, starting transfers between devices: none -> 43.6 us  [the longest x24 42.2 us: send(): return lax.ppermute(value, 'wide', moves)]
    another operation x10 -> x6, other arithmetic: 45.7 us -> 3.62 us  [the longest x2 1.69 us: on_device(): jnp.stack([packed] + [send(packed, shift(r)) for r in range(1, depth)])]
    ppermute x0 -> x30, waiting for transfers between devices: none -> 37.9 us  [the longest x24 37.9 us: send(): return lax.ppermute(value, 'wide', moves)]
    all_to_all x1 -> x0, waiting for transfers between devices: 35.8 us -> none  [on_device(): lax.all_to_all(full_width, 'wide', split_axis=1, concat_axis=0, tiled=True)]
  transfers between devices with their start and end apart: 8 -> 30, of which waited for: 8 -> 10; matrix products, arithmetic and copies ran while one was open for 3% -> 9% of each run, Pallas kernels for 0% -> 22%
where the time goes in v1:
time: 167 us
  Pallas kernels  67.4 us (40%)
  starting transfers between devices  43.6 us (26%)
  waiting for transfers between devices  37.9 us (23%)
  local copies, waits for them, and re-layouts  10.8 us (6%)
  other arithmetic  4.96 us (3%)
    ppermute x24, starting transfers between devices, send(): return lax.ppermute(value, 'wide', moves)  42.2 us
    ppermute x24, waiting for transfers between devices, send(): return lax.ppermute(value, 'wide', moves)  37.9 us
    pallas_call x1, Pallas kernels, kernel_block(): pl.pallas_call(lambda *refs: kernel_block_body(last, tile, *refs), in_spe...  31 us
    pallas_call x4, Pallas kernels, group_scan(): pl.pallas_call(group_scan_body, in_specs=[pl.BlockSpec(memory_space=pltpu...  12.6 us
    pallas_call x1, Pallas kernels, second_panel(): pl.pallas_call(second_panel_body, out_shape=(jax.ShapeDtypeStruct((PIVOTS...  10 us
    pallas_call x1, Pallas kernels, first_panel(): pl.pallas_call(lambda *refs: first_panel_body(slab, each, *refs), in_spec...  8.36 us
    pallas_call x1, Pallas kernels, early_rows(): pl.pallas_call(body, in_specs=[pl.BlockSpec(memory_space=pltpu.SMEM)] + [...  5.43 us
    slice x4, local copies, waits for them, and re-layouts, on_device(): diag_b = send(across_x[:, half:], swap_y)  3.84 us
  transfers between devices with their start and end apart: 30, of which 10 were waited for; matrix products, arithmetic and copies ran while one was open for 9% of the time, Pallas kernels for 22%

profile of v1, /device:TPU:0, one launch (start us, length us, event | category | flops | bytes accessed | tf_op | source)
XLA Modules:
  0.0 166.9 jit_solution(12470101410761003772)
XLA Ops:
  0.6 3.1 %collective-permute-start.11 = (bf16[32,8192]{1,0:T(8,128)(2,1)}, bf16[32,8192]{1,0:T(8,128)(2,1)}, u32[]{:S(2)}, u32[]{:S(2)}) collective-permute-start(bf16[32,8192]{1,0:T(8,128)(2,1)} %refs_9_.1), channel_id=1, source_target_pairs={{0,8},{2,10},{4,12},{6,14},{8,16},{10,18},{12,20},{14,22},{16,24},... | collective-permute-start | bytes 1572872 | tf_op jit(solution)/shard_map/ppermute | solution.py:310
  5.3 1.6 collective-permute-start
  6.9 2.3 %collective-permute-done = bf16[48,256]{1,0:T(8,128)(2,1)S(1)} collective-permute-done((bf16[48,256]{1,0:T(8,128)(2,1)S(1)}, bf16[48,256]{1,0:T(8,128)(2,1)S(1)}, u32[]{:S(2)}, u32[]{:S(2)}) %collective-permute-start) | collective-permute-done | bytes 24608 | tf_op jit(solution)/shard_map/ppermute | solution.py:310
  9.2 1.5 collective-permute-start.1
  10.8 2.6 %collective-permute-done.1 = bf16[2,48,256]{2,1,0:T(8,128)(2,1)S(1)} collective-permute-done((bf16[2,48,256]{2,1,0:T(8,128)(2,1)S(1)}, bf16[2,48,256]{2,1,0:T(8,128)(2,1)S(1)}, u32[]{:S(2)}, u32[]{:S(2)}) %collective-permute-start.1) | collective-permute-done | bytes 49184 | tf_op jit(solution)/shard_map/ppermute | solution.py:310
  14.0 2.6 %collective-permute-start.3 = (bf16[4,48,256]{2,1,0:T(8,128)(2,1)}, bf16[4,48,256]{2,1,0:T(8,128)(2,1)}, u32[]{:S(2)}, u32[]{:S(2)}) collective-permute-start(bf16[4,48,256]{2,1,0:T(8,128)(2,1)} %get-tuple-element.40), channel_id=1, source_target_pairs={{0,16},{2,18},{4,20},{6,22},{8,24},{10,26},{12,28},{14,30},{16,0},... | collective-permute-start | bytes 294920 | tf_op jit(solution)/shard_map/ppermute | solution.py:310
  16.6 1.5 collective-permute-start.7
  22.3 10.3 %collective-permute-start.2 = (bf16[4,48,256]{2,1,0:T(8,128)(2,1)}, bf16[4,48,256]{2,1,0:T(8,128)(2,1)}, u32[]{:S(2)}, u32[]{:S(2)}) collective-permute-start(bf16[4,48,256]{2,1,0:T(8,128)(2,1)} %get-tuple-element.40), channel_id=1, source_target_pairs={{0,8},{2,10},{4,12},{6,14},{8,16},{10,18},{12,20},{14,22},{16,24},... | collective-permute-start | bytes 294920 | tf_op jit(solution)/shard_map/ppermute | solution.py:310
  32.6 6.6 %collective-permute-done.2 = bf16[4,48,256]{2,1,0:T(8,128)(2,1)} collective-permute-done((bf16[4,48,256]{2,1,0:T(8,128)(2,1)}, bf16[4,48,256]{2,1,0:T(8,128)(2,1)}, u32[]{:S(2)}, u32[]{:S(2)}) %collective-permute-start.2) | collective-permute-done | bytes 98336 | tf_op jit(solution)/shard_map/ppermute | solution.py:310
  39.2 1.6 collective-permute-start.13
  40.9 1.5 collective-permute-start.12
  42.4 2.8 %collective-permute-done.17.own_ref.refs_24_ = bf16[32,8192]{1,0:T(8,128)(2,1)S(1)} collective-permute-done((bf16[32,8192]{1,0:T(8,128)(2,1)}, bf16[32,8192]{1,0:T(8,128)(2,1)S(1)}, u32[]{:S(2)}, u32[]{:S(2)}) %collective-permute-start.17) | collective-permute-done | bytes 524320 | tf_op jit(solution)/shard_map/ppermute | solution.py:310
  45.2 1.7 collective-permute-start.18
  46.9 2.9 %collective-permute-start.25 = (bf16[32,8192]{1,0:T(8,128)(2,1)}, bf16[32,8192]{1,0:T(8,128)(2,1)}, u32[]{:S(2)}, u32[]{:S(2)}) collective-permute-start(bf16[32,8192]{1,0:T(8,128)(2,1)} %collective-permute-done.23.own_ref.refs_19_), channel_id=1, source_target_pairs={{0,4},{2,6},{4,0},{6,2},{8,12},{10,14},{12,8},{14,10},{16,20},{18,... | collective-permute-start | bytes 1572872 | tf_op jit(solution)/shard_map/ppermute | solution.py:310
  49.8 4.4 %collective-permute-done.13.y_ref.refs_16_ = bf16[32,8192]{1,0:T(8,128)(2,1)S(1)} collective-permute-done((bf16[32,8192]{1,0:T(8,128)(2,1)}, bf16[32,8192]{1,0:T(8,128)(2,1)S(1)}, u32[]{:S(2)}, u32[]{:S(2)}) %collective-permute-start.13) | collective-permute-done | bytes 524320 | tf_op jit(solution)/shard_map/ppermute | solution.py:310
  57.8 7.7 %collective-permute-done.19.y_ref.refs_26_ = bf16[32,8192]{1,0:T(8,128)(2,1)S(1)} collective-permute-done((bf16[32,8192]{1,0:T(8,128)(2,1)S(1)}, bf16[32,8192]{1,0:T(8,128)(2,1)S(1)}, u32[]{:S(2)}, u32[]{:S(2)}) %collective-permute-start.19) | collective-permute-done | bytes 524320 | tf_op jit(solution)/shard_map/ppermute | solution.py:310
  65.5 1.6 collective-permute-start.9
  67.1 1.6 collective-permute-start.14
  69.4 7.4 %collective-permute-done.25.y_ref.refs_21_ = bf16[32,8192]{1,0:T(8,128)(2,1)} collective-permute-done((bf16[32,8192]{1,0:T(8,128)(2,1)}, bf16[32,8192]{1,0:T(8,128)(2,1)}, u32[]{:S(2)}, u32[]{:S(2)}) %collective-permute-start.25) | collective-permute-done | bytes 524320 | tf_op jit(solution)/shard_map/ppermute | solution.py:310
  78.5 2.0 %collective-permute-start.15 = (bf16[32,4096]{1,0:T(8,128)(2,1)}, bf16[32,4096]{1,0:T(8,128)(2,1)}, u32[]{:S(2)}, u32[]{:S(2)}) collective-permute-start(bf16[32,4096]{1,0:T(8,128)(2,1)} %slice.43), channel_id=1, source_target_pairs={{0,4},{2,6},{4,0},{6,2},{8,12},{10,14},{12,8},{14,10},{16,20},{18,... | collective-permute-start | bytes 786440 | tf_op jit(solution)/shard_map/ppermute | solution.py:310
  82.0 1.7 %slice.46 = bf16[32,4096]{1,0:T(8,128)(2,1)} slice(bf16[32,8192]{1,0:T(8,128)(2,1)} %collective-permute-done.25.y_ref.refs_21_), slice={[0:32], [0:4096]} | slice | bytes 524288 | tf_op jit(solution)/shard_map/slice | solution.py:355
  83.7 1.7 slice.47
  85.3 1.6 collective-permute-start.20
  87.5 2.2 %collective-permute-done.14.a_ref.refs_17_ = bf16[32,4096]{1,0:T(8,128)(2,1)} collective-permute-done((bf16[32,4096]{1,0:T(8,128)(2,1)S(1)}, bf16[32,4096]{1,0:T(8,128)(2,1)}, u32[]{:S(2)}, u32[]{:S(2)}) %collective-permute-start.14) | collective-permute-done | bytes 262176 | tf_op jit(solution)/shard_map/ppermute | solution.py:310
  92.5 3.1 %group_scan.4 = (f32[128,64]{1,0:T(8,128)}, bf16[128,1024]{1,0:T(8,128)(2,1)}) custom-call(s32[2]{0:T(128)} %pad_add_fusion.1.home_ref, bf16[64,8192]{1,0:T(8,128)(2,1)} %queries_ref.7, bf16[32,8192]{1,0:T(8,128)(2,1)} %refs_9_.1, bf16[32,8192]{1,0:T(8,128)(2,1)} %copy-done.2, bf16[32,8192]{1,0:T(8,128)(2,1)} %copy-done.1, ...), custom_call_target="tpu_custom_call" | custom-call | tf_op jit(solution)/shard_map/group_scan/pallas_call | solution.py:152
  95.7 3.2 %group_scan.5 = (f32[128,64]{1,0:T(8,128)}, bf16[128,1024]{1,0:T(8,128)(2,1)}) custom-call(s32[2]{0:T(128)} %pad_add_fusion.1.home_ref, bf16[64,8192]{1,0:T(8,128)(2,1)} %queries_ref.7, bf16[32,8192]{1,0:T(8,128)(2,1)} %collective-permute-done.11.own_ref.refs_14_, bf16[32,8192]{1,0:T(8,128)(2,1)} %copy-done.4, bf16[32,8192]{1,0:T(8,128)(2,1)} %copy-done.3, ...), custom_call_target="tpu_custom_call" | custom-call | tf_op jit(solution)/shard_map/group_scan/pallas_call | solution.py:152
  100.2 3.1 %group_scan.6 = (f32[128,64]{1,0:T(8,128)}, bf16[128,1024]{1,0:T(8,128)(2,1)}) custom-call(s32[2]{0:T(128)} %pad_add_fusion.1.home_ref, bf16[64,8192]{1,0:T(8,128)(2,1)} %queries_ref.7, bf16[32,8192]{1,0:T(8,128)(2,1)} %copy-done.7, bf16[32,8192]{1,0:T(8,128)(2,1)} %copy-done.6, bf16[32,8192]{1,0:T(8,128)(2,1)} %copy-done.5, bf16[32,4096]{1,0:T(8,128)(2,1)} %copy-done.13, ...), custom_call_target="tpu_custom_call" | custom-call | tf_op jit(solution)/shard_map/group_scan/pallas_call | solution.py:152
  104.1 3.1 %group_scan.7 = (f32[128,64]{1,0:T(8,128)}, bf16[128,1024]{1,0:T(8,128)(2,1)}) custom-call(s32[2]{0:T(128)} %pad_add_fusion.1.home_ref, bf16[64,8192]{1,0:T(8,128)(2,1)} %queries_ref.7, bf16[32,8192]{1,0:T(8,128)(2,1)} %collective-permute-done.23.own_ref.refs_19_, bf16[32,8192]{1,0:T(8,128)(2,1)} %collective-permute-done.24.x_ref.refs_20_, ...), custom_call_target="tpu_custom_call" | custom-call | tf_op jit(solution)/shard_map/group_scan/pallas_call | solution.py:152
  109.9 8.4 %first_panel.1 = (bf16[512,256]{1,0:T(8,128)(2,1)}, f32[128,128]{1,0:T(8,128)}, f32[128,128]{1,0:T(8,128)}, f32[128,128]{1,0:T(8,128)}) custom-call(s32[2]{0:T(128)} %pad_add_fusion.2.refs_0_, bf16[16,48,256]{2,1,0:T(8,128)(2,1)} %bitcast.20, bf16[16,48,256]{2,1,0:T(8,128)(2,1)} %bitcast.23), custom_call_target="tpu_custom_call" | custom-call | tf_op jit(solution)/shard_map/first_panel/pallas_call | solution.py:98
  118.3 10.0 %second_panel.1 = (f32[256,256]{1,0:T(8,128)}, bf16[3,512,512]{2,1,0:T(8,128)(2,1)}) custom-call(f32[128,128]{1,0:T(8,128)} %get-tuple-element.22.inv_ref, f32[128,128]{1,0:T(8,128)} %get-tuple-element.23.left_ref, f32[128,128]{1,0:T(8,128)} %get-tuple-element.24.rest_ref, bf16[512,256]{1,0:T(8,128)(2,1)} %get-tuple-element.21.fp_ref), custom_call_target="tpu_custom_call" | custom-call | tf_op jit(solution)/shard_map/second_panel/pallas_call | solution.py:129
  129.2 5.4 %early_rows.1 = (f32[1024,512]{1,0:T(8,128)}, f32[1024,256]{1,0:T(8,128)}) custom-call(s32[2]{0:T(128)} %pad_add_fusion.1.home_ref, bf16[4,128,256]{2,1,0:T(8,128)(2,1)} %bitcast.21, bf16[3,4,128,512]{3,2,1,0:T(8,128)(2,1)} %bitcast.18, bf16[128,1024]{1,0:T(8,128)(2,1)} %get-tuple-element.26.refs_0_, bf16[128,1024]{1,0:T(8,128)(2,1)} %copy-done.10, ...), custom_call_target="tpu_custom_call" | custom-call | tf_op jit(solution)/shard_map/early_rows/pallas_call | solution.py:180
  135.9 31.0 %kernel_block.1 = (f32[1024,8192]{1,0:T(8,128)}, f32[1024,256]{1,0:T(8,128)}) custom-call(s32[3]{0:T(128)} %pad_add_fusion.refs_0_, f32[1,1024]{1,0:T(1,128)} %bitcast.28, f32[1024,512]{1,0:T(8,128)} %get-tuple-element.29.refs_2_, f32[1024,256]{1,0:T(8,128)} %get-tuple-element.30.refs_3_, bf16[4,128,256]{2,1,0:T(8,128)(2,1)} %bitcast.22, ...), custom_call_target="tpu_custom_call" | custom-call | flops 17179869184 | bytes 41943040 | tf_op jit(solution)/shard_map/kernel_block/pallas_call | solution.py:268
  (101 shorter events, 24.2 us)
Async XLA Ops:
  0.6 32.0 %collective-permute-start.11 = (bf16[32,8192]{1,0:T(8,128)(2,1)}, bf16[32,8192]{1,0:T(8,128)(2,1)}, u32[]{:S(2)}, u32[]{:S(2)}) collective-permute-start(bf16[32,8192]{1,0:T(8,128)(2,1)} %refs_9_.1), channel_id=1, source_target_pairs={{0,8},{2,10},{4,12},{6,14},{8,16},{10,18},{12,20},{14,22},{16,24},... | collective-permute-start | bytes 1572872 | tf_op jit(solution)/shard_map/ppermute | solution.py:310
  5.3 3.9 %collective-permute-start = (bf16[48,256]{1,0:T(8,128)(2,1)S(1)}, bf16[48,256]{1,0:T(8,128)(2,1)S(1)}, u32[]{:S(2)}, u32[]{:S(2)}) collective-permute-start(bf16[48,256]{1,0:T(8,128)(2,1)S(1)} %concatenate.10), channel_id=1, source_target_pairs={{0,2},{2,0},{4,6},{6,4},{8,10},{10,8},{12,14},{14,12},{16,18},{18,... | collective-permute-start | bytes 73736 | tf_op jit(solution)/shard_map/ppermute | solution.py:310
  9.2 4.1 %collective-permute-start.1 = (bf16[2,48,256]{2,1,0:T(8,128)(2,1)S(1)}, bf16[2,48,256]{2,1,0:T(8,128)(2,1)S(1)}, u32[]{:S(2)}, u32[]{:S(2)}) collective-permute-start(bf16[2,48,256]{2,1,0:T(8,128)(2,1)S(1)} %pad_maximum_fusion.2), channel_id=1, source_target_pairs={{0,4},{2,6},{4,0},{6,2},{8,12},{10,14},{12,8},{14,10},{16,20},{18,... | collective-permute-start | bytes 147464 | tf_op jit(solution)/shard_map/ppermute | solution.py:310
  14.0 8.3 %collective-permute-start.3 = (bf16[4,48,256]{2,1,0:T(8,128)(2,1)}, bf16[4,48,256]{2,1,0:T(8,128)(2,1)}, u32[]{:S(2)}, u32[]{:S(2)}) collective-permute-start(bf16[4,48,256]{2,1,0:T(8,128)(2,1)} %get-tuple-element.40), channel_id=1, source_target_pairs={{0,16},{2,18},{4,20},{6,22},{8,24},{10,26},{12,28},{14,30},{16,0},... | collective-permute-start | bytes 294920 | tf_op jit(solution)/shard_map/ppermute | solution.py:310
  16.6 24.3 %collective-permute-start.7 = (bf16[32,8192]{1,0:T(8,128)(2,1)}, bf16[32,8192]{1,0:T(8,128)(2,1)S(1)}, u32[]{:S(2)}, u32[]{:S(2)}) collective-permute-start(bf16[32,8192]{1,0:T(8,128)(2,1)} %refs_9_.1), channel_id=1, source_target_pairs={{0,4},{2,6},{4,0},{6,2},{8,12},{10,14},{12,8},{14,10},{16,20},{18,... | collective-permute-start | bytes 1572872 | tf_op jit(solution)/shard_map/ppermute | solution.py:310
  18.1 27.1 %collective-permute-start.17 = (bf16[32,8192]{1,0:T(8,128)(2,1)}, bf16[32,8192]{1,0:T(8,128)(2,1)S(1)}, u32[]{:S(2)}, u32[]{:S(2)}) collective-permute-start(bf16[32,8192]{1,0:T(8,128)(2,1)} %refs_9_.1), channel_id=1, source_target_pairs={{0,24},{2,26},{4,28},{6,30},{8,0},{10,2},{12,4},{14,6},{16,8},{18,... | collective-permute-start | bytes 1572872 | tf_op jit(solution)/shard_map/ppermute | solution.py:310
  19.4 25.8 %collective-permute-start.6 = (bf16[32,8192]{1,0:T(8,128)(2,1)}, bf16[32,8192]{1,0:T(8,128)(2,1)S(1)}, u32[]{:S(2)}, u32[]{:S(2)}) collective-permute-start(bf16[32,8192]{1,0:T(8,128)(2,1)} %refs_9_.1), channel_id=1, source_target_pairs={{0,2},{2,0},{4,6},{6,4},{8,10},{10,8},{12,14},{14,12},{16,18},{18,... | collective-permute-start | bytes 1572872 | tf_op jit(solution)/shard_map/ppermute | solution.py:310
  22.3 16.9 %collective-permute-start.2 = (bf16[4,48,256]{2,1,0:T(8,128)(2,1)}, bf16[4,48,256]{2,1,0:T(8,128)(2,1)}, u32[]{:S(2)}, u32[]{:S(2)}) collective-permute-start(bf16[4,48,256]{2,1,0:T(8,128)(2,1)} %get-tuple-element.40), channel_id=1, source_target_pairs={{0,8},{2,10},{4,12},{6,14},{8,16},{10,18},{12,20},{14,22},{16,24},... | collective-permute-start | bytes 294920 | tf_op jit(solution)/shard_map/ppermute | solution.py:310
  32.6 14.3 %collective-permute-start.23 = (bf16[32,8192]{1,0:T(8,128)(2,1)}, bf16[32,8192]{1,0:T(8,128)(2,1)}, u32[]{:S(2)}, u32[]{:S(2)}) collective-permute-start(bf16[32,8192]{1,0:T(8,128)(2,1)} %collective-permute-done.11.own_ref.refs_14_), channel_id=1, source_target_pairs={{0,8},{2,10},{4,12},{6,14},{8,16},{10,18},{12,20},{14,22},{16,24},... | collective-permute-start | bytes 1572872 | tf_op jit(solution)/shard_map/ppermute | solution.py:310
  39.2 15.0 %collective-permute-start.13 = (bf16[32,8192]{1,0:T(8,128)(2,1)}, bf16[32,8192]{1,0:T(8,128)(2,1)S(1)}, u32[]{:S(2)}, u32[]{:S(2)}) collective-permute-start(bf16[32,8192]{1,0:T(8,128)(2,1)} %collective-permute-done.11.own_ref.refs_14_), channel_id=1, source_target_pairs={{0,4},{2,6},{4,0},{6,2},{8,12},{10,14},{12,8},{14,10},{16,20},{18,... | collective-permute-start | bytes 1572872 | tf_op jit(solution)/shard_map/ppermute | solution.py:310
  40.9 44.5 %copy-start.1 = (bf16[32,8192]{1,0:T(8,128)(2,1)}, bf16[32,8192]{1,0:T(8,128)(2,1)S(1)}, u32[]{:S(2)}) copy-start(bf16[32,8192]{1,0:T(8,128)(2,1)S(1)} %collective-permute-done.7.y_ref.refs_11_) | copy-start | bytes 1572868
  40.9 16.3 %collective-permute-start.12 = (bf16[32,8192]{1,0:T(8,128)(2,1)}, bf16[32,8192]{1,0:T(8,128)(2,1)S(1)}, u32[]{:S(2)}, u32[]{:S(2)}) collective-permute-start(bf16[32,8192]{1,0:T(8,128)(2,1)} %collective-permute-done.11.own_ref.refs_14_), channel_id=1, source_target_pairs={{0,2},{2,0},{4,6},{6,4},{8,10},{10,8},{12,14},{14,12},{16,18},{18,... | collective-permute-start | bytes 1572872 | tf_op jit(solution)/shard_map/ppermute | solution.py:310
  45.2 20.3 %collective-permute-start.19 = (bf16[32,8192]{1,0:T(8,128)(2,1)S(1)}, bf16[32,8192]{1,0:T(8,128)(2,1)S(1)}, u32[]{:S(2)}, u32[]{:S(2)}) collective-permute-start(bf16[32,8192]{1,0:T(8,128)(2,1)S(1)} %collective-permute-done.17.own_ref.refs_24_), channel_id=1, source_target_pairs={{0,4},{2,6},{4,0},{6,2},{8,12},{10,14},{12,8},{14,10},{16,20},{18,... | collective-permute-start | bytes 1572872 | tf_op jit(solution)/shard_map/ppermute | solution.py:310
  45.2 40.1 %copy-start.2 = (bf16[32,8192]{1,0:T(8,128)(2,1)}, bf16[32,8192]{1,0:T(8,128)(2,1)S(1)}, u32[]{:S(2)}) copy-start(bf16[32,8192]{1,0:T(8,128)(2,1)S(1)} %collective-permute-done.6.x_ref.refs_10_) | copy-start | bytes 1572868
  45.2 21.9 %collective-permute-start.18 = (bf16[32,8192]{1,0:T(8,128)(2,1)S(1)}, bf16[32,8192]{1,0:T(8,128)(2,1)S(1)}, u32[]{:S(2)}, u32[]{:S(2)}) collective-permute-start(bf16[32,8192]{1,0:T(8,128)(2,1)S(1)} %collective-permute-done.17.own_ref.refs_24_), channel_id=1, source_target_pairs={{0,2},{2,0},{4,6},{6,4},{8,10},{10,8},{12,14},{14,12},{16,18},{18,... | collective-permute-start | bytes 1572872 | tf_op jit(solution)/shard_map/ppermute | solution.py:310
  46.9 29.9 %collective-permute-start.25 = (bf16[32,8192]{1,0:T(8,128)(2,1)}, bf16[32,8192]{1,0:T(8,128)(2,1)}, u32[]{:S(2)}, u32[]{:S(2)}) collective-permute-start(bf16[32,8192]{1,0:T(8,128)(2,1)} %collective-permute-done.23.own_ref.refs_19_), channel_id=1, source_target_pairs={{0,4},{2,6},{4,0},{6,2},{8,12},{10,14},{12,8},{14,10},{16,20},{18,... | collective-permute-start | bytes 1572872 | tf_op jit(solution)/shard_map/ppermute | solution.py:310
  54.2 24.2 %collective-permute-start.24 = (bf16[32,8192]{1,0:T(8,128)(2,1)}, bf16[32,8192]{1,0:T(8,128)(2,1)}, u32[]{:S(2)}, u32[]{:S(2)}) collective-permute-start(bf16[32,8192]{1,0:T(8,128)(2,1)} %collective-permute-done.23.own_ref.refs_19_), channel_id=1, source_target_pairs={{0,2},{2,0},{4,6},{6,4},{8,10},{10,8},{12,14},{14,12},{16,18},{18,... | collective-permute-start | bytes 1572872 | tf_op jit(solution)/shard_map/ppermute | solution.py:310
  57.2 29.7 %collective-permute-start.8 = (bf16[32,4096]{1,0:T(8,128)(2,1)}, bf16[32,4096]{1,0:T(8,128)(2,1)}, u32[]{:S(2)}, u32[]{:S(2)}) collective-permute-start(bf16[32,4096]{1,0:T(8,128)(2,1)} %slice.40), channel_id=1, source_target_pairs={{0,2},{2,0},{4,6},{6,4},{8,10},{10,8},{12,14},{14,12},{16,18},{18,... | collective-permute-start | bytes 786440 | tf_op jit(solution)/shard_map/ppermute | solution.py:310
  65.5 21.4 %collective-permute-start.9 = (bf16[32,4096]{1,0:T(8,128)(2,1)}, bf16[32,4096]{1,0:T(8,128)(2,1)}, u32[]{:S(2)}, u32[]{:S(2)}) collective-permute-start(bf16[32,4096]{1,0:T(8,128)(2,1)} %slice.41), channel_id=1, source_target_pairs={{0,4},{2,6},{4,0},{6,2},{8,12},{10,14},{12,8},{14,10},{16,20},{18,... | collective-permute-start | bytes 786440 | tf_op jit(solution)/shard_map/ppermute | solution.py:310
  67.1 22.6 %collective-permute-start.14 = (bf16[32,4096]{1,0:T(8,128)(2,1)S(1)}, bf16[32,4096]{1,0:T(8,128)(2,1)}, u32[]{:S(2)}, u32[]{:S(2)}) collective-permute-start(bf16[32,4096]{1,0:T(8,128)(2,1)S(1)} %slice.42), channel_id=1, source_target_pairs={{0,2},{2,0},{4,6},{6,4},{8,10},{10,8},{12,14},{14,12},{16,18},{18,... | collective-permute-start | bytes 786440 | tf_op jit(solution)/shard_map/ppermute | solution.py:310
  76.8 8.5 %collective-permute-start.4 = (bf16[4,48,256]{2,1,0:T(8,128)(2,1)}, bf16[4,48,256]{2,1,0:T(8,128)(2,1)}, u32[]{:S(2)}, u32[]{:S(2)}) collective-permute-start(bf16[4,48,256]{2,1,0:T(8,128)(2,1)} %get-tuple-element.40), channel_id=1, source_target_pairs={{0,24},{2,26},{4,28},{6,30},{8,0},{10,2},{12,4},{14,6},{16,8},{18,... | collective-permute-start | bytes 294920 | tf_op jit(solution)/shard_map/ppermute | solution.py:310
  78.5 13.3 %collective-permute-start.15 = (bf16[32,4096]{1,0:T(8,128)(2,1)}, bf16[32,4096]{1,0:T(8,128)(2,1)}, u32[]{:S(2)}, u32[]{:S(2)}) collective-permute-start(bf16[32,4096]{1,0:T(8,128)(2,1)} %slice.43), channel_id=1, source_target_pairs={{0,4},{2,6},{4,0},{6,2},{8,12},{10,14},{12,8},{14,10},{16,20},{18,... | collective-permute-start | bytes 786440 | tf_op jit(solution)/shard_map/ppermute | solution.py:310
  85.3 13.5 %collective-permute-start.20 = (bf16[32,4096]{1,0:T(8,128)(2,1)}, bf16[32,4096]{1,0:T(8,128)(2,1)S(1)}, u32[]{:S(2)}, u32[]{:S(2)}) collective-permute-start(bf16[32,4096]{1,0:T(8,128)(2,1)} %slice.44), channel_id=1, source_target_pairs={{0,2},{2,0},{4,6},{6,4},{8,10},{10,8},{12,14},{14,12},{16,18},{18,... | collective-permute-start | bytes 786440 | tf_op jit(solution)/shard_map/ppermute | solution.py:310
  86.9 12.5 %collective-permute-start.21 = (bf16[32,4096]{1,0:T(8,128)(2,1)}, bf16[32,4096]{1,0:T(8,128)(2,1)S(1)}, u32[]{:S(2)}, u32[]{:S(2)}) collective-permute-start(bf16[32,4096]{1,0:T(8,128)(2,1)} %slice.45), channel_id=1, source_target_pairs={{0,4},{2,6},{4,0},{6,2},{8,12},{10,14},{12,8},{14,10},{16,20},{18,... | collective-permute-start | bytes 786440 | tf_op jit(solution)/shard_map/ppermute | solution.py:310
  86.9 16.4 %collective-permute-start.26 = (bf16[32,4096]{1,0:T(8,128)(2,1)}, bf16[32,4096]{1,0:T(8,128)(2,1)}, u32[]{:S(2)}, u32[]{:S(2)}) collective-permute-start(bf16[32,4096]{1,0:T(8,128)(2,1)} %slice.46), channel_id=1, source_target_pairs={{0,2},{2,0},{4,6},{6,4},{8,10},{10,8},{12,14},{14,12},{16,18},{18,... | collective-permute-start | bytes 786440 | tf_op jit(solution)/shard_map/ppermute | solution.py:310
  89.7 13.7 %collective-permute-start.27 = (bf16[32,4096]{1,0:T(8,128)(2,1)}, bf16[32,4096]{1,0:T(8,128)(2,1)S(1)}, u32[]{:S(2)}, u32[]{:S(2)}) collective-permute-start(bf16[32,4096]{1,0:T(8,128)(2,1)} %slice.47), channel_id=1, source_target_pairs={{0,4},{2,6},{4,0},{6,2},{8,12},{10,14},{12,8},{14,10},{16,20},{18,... | collective-permute-start | bytes 786440 | tf_op jit(solution)/shard_map/ppermute | solution.py:310
  91.8 17.4 %collective-permute-start.5 = (bf16[4,4,48,256]{3,2,1,0:T(8,128)(2,1)S(1)}, bf16[4,4,48,256]{3,2,1,0:T(8,128)(2,1)S(1)}, u32[]{:S(2)}, u32[]{:S(2)}) collective-permute-start(bf16[4,4,48,256]{3,2,1,0:T(8,128)(2,1)S(1)} %pad_maximum_fusion), channel_id=1, source_target_pairs={{0,1},{1,0},{2,3},{3,2},{4,5},{5,4},{6,7},{7,6},{8,9},{9,8},{10,11... | collective-permute-start | bytes 1179656 | tf_op jit(solution)/shard_map/ppermute | solution.py:314
  98.9 29.4 %collective-permute-start.10 = (bf16[128,1024]{1,0:T(8,128)(2,1)S(1)}, bf16[128,1024]{1,0:T(8,128)(2,1)S(1)}, u32[]{:S(2)}, u32[]{:S(2)}) collective-permute-start(bf16[128,1024]{1,0:T(8,128)(2,1)S(1)} %copy-done.9), channel_id=1, source_target_pairs={{0,1},{1,0},{2,3},{3,2},{4,5},{5,4},{6,7},{7,6},{8,9},{9,8},{10,11... | collective-permute-start | bytes 786440 | tf_op jit(solution)/shard_map/ppermute | solution.py:314
  99.4 28.9 %collective-permute-start.16 = (bf16[128,1024]{1,0:T(8,128)(2,1)}, bf16[128,1024]{1,0:T(8,128)(2,1)S(1)}, u32[]{:S(2)}, u32[]{:S(2)}) collective-permute-start(bf16[128,1024]{1,0:T(8,128)(2,1)} %get-tuple-element.27.refs_2_), channel_id=1, source_target_pairs={{0,1},{1,0},{2,3},{3,2},{4,5},{5,4},{6,7},{7,6},{8,9},{9,8},{10,11... | collective-permute-start | bytes 786440 | tf_op jit(solution)/shard_map/ppermute | solution.py:314
  103.3 25.0 %collective-permute-start.22 = (bf16[128,1024]{1,0:T(8,128)(2,1)}, bf16[128,1024]{1,0:T(8,128)(2,1)S(1)}, u32[]{:S(2)}, u32[]{:S(2)}) collective-permute-start(bf16[128,1024]{1,0:T(8,128)(2,1)} %get-tuple-element.28.refs_4_), channel_id=1, source_target_pairs={{0,1},{1,0},{2,3},{3,2},{4,5},{5,4},{6,7},{7,6},{8,9},{9,8},{10,11... | collective-permute-start | bytes 786440 | tf_op jit(solution)/shard_map/ppermute | solution.py:314
  107.2 28.0 %collective-permute-start.28 = (bf16[128,1024]{1,0:T(8,128)(2,1)}, bf16[128,1024]{1,0:T(8,128)(2,1)S(1)}, u32[]{:S(2)}, u32[]{:S(2)}) collective-permute-start(bf16[128,1024]{1,0:T(8,128)(2,1)} %get-tuple-element.32.refs_7_), channel_id=1, source_target_pairs={{0,1},{1,0},{2,3},{3,2},{4,5},{5,4},{6,7},{7,6},{8,9},{9,8},{10,11... | collective-permute-start | bytes 786440 | tf_op jit(solution)/shard_map/ppermute | solution.py:314
  109.2 25.4 %collective-permute-start.29 = (f32[64,256]{1,0:T(8,128)S(1)}, f32[64,256]{1,0:T(8,128)S(1)}, u32[]{:S(2)}, u32[]{:S(2)}) collective-permute-start(f32[64,256]{1,0:T(8,128)S(1)} %constant_dynamic-slice_fusion), channel_id=1, source_target_pairs={{0,1},{1,0},{2,3},{3,2},{4,5},{5,4},{6,7},{7,6},{8,9},{9,8},{10,11... | collective-permute-start | bytes 196616 | tf_op jit(solution)/shard_map/ppermute | solution.py:385
  (18 other events, 179.7 us)

commit v2 on v1

v2 whole, which is shorter than its diff:
```python
import math

import jax
import jax.numpy as jnp
from jax import lax
from jax.experimental import pallas as pl
from jax.experimental.pallas import tpu as pltpu
from jax.sharding import PartitionSpec as P


PANEL = 128
PANELS = 2
PIVOTS = PANEL * PANELS
TILE = 512
SLOTS = 4
HIGHEST = lax.Precision.HIGHEST


def dot(a, b, ca, cb, precision=None):
    return lax.dot_general(
        a, b, (((ca,), (cb,)), ((), ())), precision=precision, preferred_element_type=jnp.float32
    )


def split_bf16(value, parts):
    pieces = []
    for _ in range(parts):
        piece = lax.reduce_precision(value, 8, 7)
        pieces.append(piece.astype(jnp.bfloat16))
        value = value - piece
    return pieces


def inverse_factor(block, a_s, w_s):
    n = block.shape[0]
    sub = lax.broadcasted_iota(jnp.int32, (n, n), 0)
    lane = lax.broadcasted_iota(jnp.int32, (n, n), 1)
    lane8 = lax.broadcasted_iota(jnp.int32, (8, n), 1)
    sub8 = lax.broadcasted_iota(jnp.int32, (8, 1), 0)
    sub_col = lax.broadcasted_iota(jnp.int32, (n, 1), 0)
    a_s[...] = block
    w_s[...] = jnp.where(sub == lane, 1.0, 0.0)

    def step(b, carry):
        k0 = pl.multiple_of(b * 8, 8)
        rows = a_s[pl.ds(k0, 8), :]
        wrows = w_s[pl.ds(k0, 8), :]
        a = a_s[...]
        heads = [jnp.sum(jnp.where(lane8 == k0 + j, rows, 0.0), axis=1, keepdims=True) for j in range(8)]
        columns = [jnp.sum(jnp.where(lane == k0 + j, a, 0.0), axis=1, keepdims=True) for j in range(8)]
        scaled = []
        for j in range(8):
            inv = 1.0 / heads[j][j : j + 1, :]
            times = jnp.where(sub8 > j, heads[j], 0.0) * inv
            for m in range(j + 1, 8):
                entry = heads[m][j : j + 1, :]
                columns[m] = columns[m] - columns[j] * (entry * inv)
                heads[m] = heads[m] - times * entry
            scaled.append((rows[j : j + 1, :] * inv, wrows[j : j + 1, :] * inv))
            rows = rows - times * rows[j : j + 1, :]
            wrows = wrows - times * wrows[j : j + 1, :]
        w = w_s[...]
        for j in range(8):
            column = jnp.where(sub_col > k0 + 7, columns[j], 0.0)
            a = a - column * scaled[j][0]
            w = w - column * scaled[j][1]
        a_s[...] = a
        w_s[...] = w
        a_s[pl.ds(k0, 8), :] = rows
        w_s[pl.ds(k0, 8), :] = wrows
        return carry

    lax.fori_loop(0, n // 8, step, 0)
    diagonal = jnp.sum(jnp.where(sub == lane, a_s[...], 0.0), axis=1, keepdims=True)
    return w_s[...] * (1.0 / jnp.sqrt(diagonal))


def first_panel_body(slab, each, place_ref, packed_ref, other_ref, fp_ref, inv_ref, left_ref, rest_ref, a_s, w_s):
    mine = place_ref[1] == 0
    fp = jnp.where(mine, packed_ref[:, :each, :], other_ref[:, :each, :]).reshape(slab, PIVOTS)
    fp_ref[...] = fp
    tail = pl.ds(each, 16)
    tail = jnp.where(mine, packed_ref[place_ref[0], tail, :], other_ref[place_ref[0], tail, :])
    tail = tail.astype(jnp.float32)
    damping = tail[0:1, :] + tail[1:2, :] + tail[2:3, :]
    sub = lax.broadcasted_iota(jnp.int32, (PIVOTS, PIVOTS), 0)
    lane = lax.broadcasted_iota(jnp.int32, (PIVOTS, PIVOTS), 1)
    pivots = dot(fp, fp, 0, 0) / slab + jnp.where(sub == lane, damping, 0.0)
    inv = inverse_factor(pivots[:PANEL, :PANEL], a_s, w_s)
    left = dot(pivots[PANEL:, :PANEL], inv, 1, 1, HIGHEST)
    inv_ref[...] = inv
    left_ref[...] = left
    rest_ref[...] = pivots[PANEL:, PANEL:] - dot(left, left, 1, 1, HIGHEST)


def first_panel(place, packed, other, slab, each):
    f32 = jax.ShapeDtypeStruct((PANEL, PANEL), jnp.float32)
    return pl.pallas_call(
        lambda *refs: first_panel_body(slab, each, *refs),
        in_specs=[pl.BlockSpec(memory_space=pltpu.SMEM), pl.BlockSpec(memory_space=pltpu.VMEM)]
        + [pl.BlockSpec(memory_space=pltpu.VMEM)],
        out_shape=(jax.ShapeDtypeStruct((slab, PIVOTS), jnp.bfloat16), f32, f32, f32),
        scratch_shapes=[pltpu.VMEM((PANEL, PANEL), jnp.float32)] * 2,
        name="first_panel",
    )(place, packed, other)


def second_panel_body(damp_ref, inv_ref, left_ref, rest_ref, fp_ref, pivot_ref, factors_ref, a_s, w_s):
    slab = fp_ref.shape[0]
    first = inv_ref[...]
    inv = inverse_factor(rest_ref[...], a_s, w_s)
    below = -dot(dot(inv, left_ref[...], 1, 0, HIGHEST), first, 1, 0, HIGHEST)
    top = jnp.concatenate([first, jnp.zeros((PANEL, PANEL), jnp.float32)], axis=1)
    full = jnp.concatenate([top, jnp.concatenate([below, inv], axis=1)], axis=0)
    pivot_ref[...] = (full * damp_ref[:, :PIVOTS]).T
    basis = dot(fp_ref[...].astype(jnp.float32), full, 1, 1, HIGHEST)
    sub = lax.broadcasted_iota(jnp.int32, (slab, slab), 0)
    lane = lax.broadcasted_iota(jnp.int32, (slab, slab), 1)
    middle = jnp.where(sub == lane, 1.0, 0.0) - dot(basis, basis, 1, 1, HIGHEST) / slab
    factors = jnp.concatenate([middle, basis], axis=1)
    for part in range(3):
        piece = factors.astype(jnp.bfloat16)
        factors_ref[part] = piece
        factors = factors - piece.astype(jnp.float32)


def second_panel(damping, inv, left, rest, fp):
    slab = fp.shape[0]
    return pl.pallas_call(
        second_panel_body,
        out_shape=(
            jax.ShapeDtypeStruct((PIVOTS, PIVOTS), jnp.float32),
            jax.ShapeDtypeStruct((3, slab, slab + PIVOTS), jnp.bfloat16),
        ),
        scratch_shapes=[pltpu.VMEM((PANEL, PANEL), jnp.float32)] * 2,
        name="second_panel",
    )(damping, inv, left, rest, fp)


def own_rows_body(home_ref, *refs):
    pieces, rows_ref, sems = refs[:-2], refs[-2], refs[-1]
    rows_here = rows_ref.shape[1]
    at = pl.ds(pl.multiple_of(home_ref[0] * rows_here, 128), rows_here)
    copies = []
    begin = 0
    for k, piece in enumerate(pieces):
        size = piece.shape[0]
        copies.append(pltpu.make_async_copy(piece.at[:, at], rows_ref.at[pl.ds(begin, size), :], sems.at[k]))
        copies[-1].start()
        begin += size
    for copy in copies:
        copy.wait()


def own_rows(home, group, rows_here):
    size = sum(piece.shape[0] for piece in group)
    return pl.pallas_call(
        own_rows_body,
        in_specs=[pl.BlockSpec(memory_space=pltpu.SMEM)] + [pl.BlockSpec(memory_space=pl.ANY)] * len(group),
        out_specs=pl.BlockSpec(memory_space=pltpu.VMEM),
        out_shape=jax.ShapeDtypeStruct((size, rows_here), jnp.bfloat16),
        scratch_shapes=[pltpu.SemaphoreType.DMA((len(group),))],
        name="own_rows",
    )(home, *group)


def row_sums(home, refs, factors):
    rows = [jnp.where(home == 1, mine[...], other[...]) for mine, other in zip(*[iter(refs)] * 2)]
    rows = jnp.concatenate(rows, axis=0).T
    return dot(jnp.concatenate([rows] * 3, axis=1), jnp.concatenate(factors, axis=0), 1, 0)


def early_rows(home, at, factors, row_parts):
    rows_here = row_parts[0].shape[1]

    def body(home_ref, factors_ref, *refs):
        chosen = [factors_ref[part, a:b] for part in range(3) for a, b in at]
        refs[-1][...] = row_sums(home_ref[1], refs[:-1], chosen)

    return pl.pallas_call(
        body,
        in_specs=[pl.BlockSpec(memory_space=pltpu.SMEM)]
        + [pl.BlockSpec(memory_space=pltpu.VMEM)] * (1 + len(row_parts)),
        out_shape=jax.ShapeDtypeStruct((rows_here, factors.shape[2]), jnp.float32),
        name="early_rows",
    )(home, factors, *row_parts)


def kernel_block_body(
    at, sizes, tile, ids_ref, damp_ref, pivot_ref, early_any, factors_any, queries_any, *refs
):
    out_ref, factor_ref, scores_ref, hi_s, lo_s, factor_s, columns_s = refs[-15:-8]
    early_ref, factors_ref, queries_ref, first_sems, slots, sems, factor_sem, load_sems = refs[-8:]
    parts, pieces = refs[: 2 * len(at)], refs[2 * len(at) : -15]
    needs = [pair for entry in at for pair in entry]
    firsts = []
    spot = 0
    for a, b in needs:
        for part in range(3):
            firsts.append((factors_any.at[part, pl.ds(a, b - a)], factors_ref.at[part, pl.ds(spot, b - a)]))
        spot += b - a
    firsts += [(early_any, early_ref), (queries_any, queries_ref)]
    firsts = [pltpu.make_async_copy(*pair, first_sems.at[k]) for k, pair in enumerate(firsts)]
    for copy in firsts:
        copy.start()
    rows, slab = hi_s.shape
    cols_here = out_ref.shape[1]
    steps = cols_here // tile
    loads = []
    begin = 0
    for k, piece in enumerate(pieces):
        size, width = piece.shape
        place = columns_s.at[pl.ds(begin, size), :]
        if sizes[k]:
            offset = ids_ref[5] if sizes[k] == 1 else (cols_here - width) - ids_ref[5]
            place = columns_s.at[pl.ds(begin, size), pl.ds(pl.multiple_of(offset, 128), width)]
        loads.append(pltpu.make_async_copy(piece, place, load_sems.at[k]))
        loads[-1].start()
        begin += size if sizes[k] != 1 else 0
    row0 = ids_ref[0]
    for copy in firsts[:-2]:
        copy.wait()
    sums = row_sums(ids_ref[2], parts, [factors_ref[part] for part in range(3)])
    for copy in firsts[-2:]:
        copy.wait()
    sums = (sums + early_ref[...]) / slab
    left = sums[:, :slab]
    hi = left.astype(jnp.bfloat16)
    hi_s[...] = hi
    lo_s[...] = (left - hi.astype(jnp.float32)).astype(jnp.bfloat16)
    factor_s[...] = sums[:, slab:]

    @pl.when(row0 < PIVOTS)
    def _():
        factor_s[:PIVOTS, :] = factor_s[:PIVOTS, :] + pivot_ref[...]

    factor_copy = pltpu.make_async_copy(factor_s, factor_ref, factor_sem)
    factor_copy.start()

    def store(step, slot):
        at = pl.ds(pl.multiple_of(step * tile, 128), tile)
        return pltpu.make_async_copy(slots.at[slot], out_ref.at[:, at], sems.at[slot])

    def one(step, carry):
        slot = lax.rem(step, SLOTS)
        col0 = ids_ref[1] + step * tile
        at = pl.ds(pl.multiple_of(step * tile, 128), tile)
        columns = columns_s[:, at]

        @pl.when(step >= SLOTS)
        def _():
            store(step - SLOTS, slot).wait()

        slots[slot] = dot(hi_s[...], columns, 1, 0) + dot(lo_s[...], columns, 1, 0)

        @pl.when((col0 < row0 + rows) & (row0 < col0 + tile))
        def _():
            row_ids = row0 + lax.broadcasted_iota(jnp.int32, (rows, tile), 0)
            col_ids = col0 + lax.broadcasted_iota(jnp.int32, (rows, tile), 1)
            own_at = pl.ds(pl.multiple_of(col0 - row0, 128), tile)
            slots[slot] = slots[slot] + jnp.where(row_ids == col_ids, damp_ref[:, own_at], 0.0)

        @pl.when(row0 < PIVOTS)
        def _():
            slots[slot, :PIVOTS, :] = jnp.zeros((PIVOTS, tile), jnp.float32)

        @pl.when(col0 < PIVOTS)
        def _():
            col_ids = col0 + lax.broadcasted_iota(jnp.int32, (1, tile), 1)
            slots[slot] = jnp.where(col_ids < PIVOTS, 0.0, slots[slot])

        store(step, slot).start()
        return carry

    for load in loads:
        load.wait()
    lax.fori_loop(0, steps, one, 0)

    partial = dot(queries_ref[...], columns_s[...], 1, 1)
    each = pieces[0].shape[0]
    depth = slab // (4 * each)
    wide = row0 // rows
    x, y, z = lax.rem(wide, 2), lax.rem(wide // 2, 2), wide // 4
    width = scores_ref.shape[2]
    spot = lax.broadcasted_iota(jnp.int32, (slab, width), 0)
    name = lax.broadcasted_iota(jnp.int32, (slab, width), 1)
    block = spot // each
    local = lax.rem(block, 4)
    plane = lax.rem(z - block // 4 + depth, depth)
    example = (plane * 4 + (y ^ (local // 2)) * 2 + (x ^ lax.rem(local, 2))) * each + lax.rem(spot, each)
    for part in range(2):
        chosen = jnp.where(example == name + ids_ref[3 + part], 1.0, 0.0)
        scores_ref[part] = dot(partial, chosen, 1, 0, HIGHEST)
    for step in range(max(0, steps - SLOTS), steps):
        store(step, step % SLOTS).wait()
    factor_copy.wait()


def kernel_block(ids, damping, early, pivot_term, factors, queries, at, row_parts, pieces, sizes):
    cols_here = pieces[0].shape[1]
    rows = row_parts[0].shape[1]
    slab = factors.shape[1]
    count = queries.shape[0]
    tile = min(TILE, rows, cols_here // 2)
    fixed = [damping, pivot_term]
    loose = [early, factors, queries]
    needs = [b - a for entry in at for a, b in entry]
    return pl.pallas_call(
        lambda *refs: kernel_block_body(at, sizes, tile, *refs),
        in_specs=[pl.BlockSpec(memory_space=pltpu.SMEM)]
        + [pl.BlockSpec(memory_space=pltpu.VMEM)] * len(fixed)
        + [pl.BlockSpec(memory_space=pl.ANY)] * len(loose)
        + [pl.BlockSpec(memory_space=pltpu.VMEM)] * len(row_parts)
        + [pl.BlockSpec(memory_space=pl.ANY)] * len(pieces),
        out_specs=(
            pl.BlockSpec(memory_space=pl.ANY),
            pl.BlockSpec(memory_space=pl.ANY),
            pl.BlockSpec(memory_space=pltpu.VMEM),
        ),
        out_shape=(
            jax.ShapeDtypeStruct((rows, cols_here), jnp.float32),
            jax.ShapeDtypeStruct((rows, PIVOTS), jnp.float32),
            jax.ShapeDtypeStruct((2, count, slab // 2), jnp.float32),
        ),
        scratch_shapes=[
            pltpu.VMEM((rows, slab), jnp.bfloat16),
            pltpu.VMEM((rows, slab), jnp.bfloat16),
            pltpu.VMEM((rows, PIVOTS), jnp.float32),
            pltpu.VMEM((slab, cols_here), jnp.bfloat16),
            pltpu.VMEM((rows, slab + PIVOTS), jnp.float32),
            pltpu.VMEM((3, sum(needs), slab + PIVOTS), jnp.bfloat16),
            pltpu.VMEM(queries.shape, jnp.bfloat16),
            pltpu.SemaphoreType.DMA((3 * len(needs) + 2,)),
            pltpu.VMEM((SLOTS, rows, tile), jnp.float32),
            pltpu.SemaphoreType.DMA((SLOTS,)),
            pltpu.SemaphoreType.DMA,
            pltpu.SemaphoreType.DMA((len(pieces),)),
        ],
        cost_estimate=pl.CostEstimate(
            flops=4 * rows * slab * cols_here,
            bytes_accessed=4 * rows * cols_here + 2 * slab * cols_here,
            transcendentals=0,
        ),
        name="kernel_block",
    )(ids, *fixed, *loose, *row_parts, *pieces)


def solution(mesh):
    wide = mesh.shape["wide"]
    narrow = mesh.shape["narrow"]
    depth = wide // 4

    def index(x, y, z):
        return z * 4 + y * 2 + x

    spots = [(x, y, z) for z in range(depth) for y in range(2) for x in range(2)]
    swap_x = [(index(x, y, z), index(1 - x, y, z)) for x, y, z in spots]
    swap_y = [(index(x, y, z), index(x, 1 - y, z)) for x, y, z in spots]

    def shift(s):
        return [(index(x, y, z), index(x, y, (z + s) % depth)) for x, y, z in spots]

    def send(value, moves):
        return lax.ppermute(value, "wide", moves)

    def from_other(value, root):
        if narrow == 2:
            return lax.ppermute(value, "narrow", [(0, 1), (1, 0)])
        mine = lax.axis_index("narrow") == root
        return lax.psum(jnp.where(mine, value, jnp.zeros_like(value)), "narrow")

    sequence = []
    for r in range(1, depth // 2 + 1):
        sequence += [r] if depth - r == r else [r, depth - r]

    def on_device(features, queries, damping):
        each, cols_here = features.shape
        rows_here = damping.shape[0]
        slab = each * wide
        w = lax.axis_index("wide")
        n = lax.axis_index("narrow")

        damp_parts = jnp.stack(split_bf16(damping[:PIVOTS], 3))
        packed = jnp.concatenate(
            [features[:, :PIVOTS], damp_parts, jnp.zeros((13, PIVOTS), jnp.bfloat16)], axis=0
        )
        packed = jnp.stack([packed, send(packed, swap_x)])
        packed = jnp.concatenate([packed, send(packed, swap_y)], axis=0)
        packed = jnp.stack([packed] + [send(packed, shift(r)) for r in range(1, depth)])
        other = from_other(packed, 0).reshape(wide, each + 16, PIVOTS)
        packed = packed.reshape(wide, each + 16, PIVOTS)
        x, y, z = w % 2, (w // 2) % 2, w // 4
        place = jnp.stack([z * 4 + y * 2 + x, n]).astype(jnp.int32)
        fp, inv, left, rest = first_panel(place, packed, other, slab, each)
        pivot_term, factors = second_panel(damping[None, :], inv, left, rest, fp)

        half = cols_here // 2
        begin = (w * rows_here) % cols_here // rows_here

        def home_half(place):
            return (place * rows_here) % cols_here // half * half

        layers = {0: features}
        direct = {}
        diagonal = {}
        turns = [0] + sequence
        for turn, r in enumerate(turns):
            if r and r <= depth // 2:
                layers[r] = send(layers[r - 1], shift(1))
            elif r:
                layers[r] = send(layers[(r + 1) % depth], shift(-1))
            across_x = send(layers[r], swap_x)
            across_y = send(layers[r], swap_y)
            direct[r] = [layers[r], across_x, across_y]
            source, moves, peer = (across_x, swap_y, w ^ 2) if turn % 2 else (across_y, swap_x, w ^ 1)
            if turn < depth - 2:
                diagonal[r] = [send(source, moves)]
                continue
            first = home_half(peer)
            near = lax.dynamic_slice_in_dim(source, first, half, axis=1)
            far = lax.dynamic_slice_in_dim(source, half - first, half, axis=1)
            diagonal[r] = [send(near, moves), send(far, moves)]

        home = (w * rows_here) // cols_here
        here = jnp.stack([begin, home == n]).astype(jnp.int32)
        parts = []
        at = []
        for some in (turns[:-1], turns[-1:]):
            group = [piece for r in some for piece in direct[r] + (diagonal[r] if r in turns[:-2] else [])]
            rows = own_rows(here, group, rows_here)
            parts.append((rows, from_other(rows, home)))
            at.append([(4 * each * r, 4 * each * r + (4 if r in turns[:-2] else 3) * each) for r in some])
        inside = begin * rows_here - home_half(w)
        late = [lax.dynamic_slice_in_dim(diagonal[r][0], inside, rows_here, axis=1) for r in turns[-2:]]
        late = jnp.concatenate(late, axis=0)
        late = (late, from_other(late, home))
        late_at = [(4 * each * r + 3 * each, 4 * each * (r + 1)) for r in turns[-2:]]
        early = early_rows(here, at[0], factors, parts[0])

        split = [n * (slab // 2), (1 - n) * (slab // 2)] if narrow == 2 else [0, slab // 2]
        ids = [w * rows_here, n * cols_here, home == n, *split, home_half(w)]
        ids = jnp.stack([jnp.asarray(i).astype(jnp.int32) for i in ids])
        columns = [piece for r in range(depth) for piece in direct[r] + diagonal[r]]
        sizes = [s for r in range(depth) for s in ([0] * 4 if r in turns[:-2] else [0, 0, 0, 1, 2])]
        kernel, factor, partial = kernel_block(
            ids,
            damping[None, :],
            early,
            pivot_term,
            factors,
            queries,
            [at[1], late_at],
            [*parts[1], *late],
            columns,
            sizes,
        )
        scale = 1.0 / math.sqrt(cols_here * narrow)
        if narrow == 2:
            other = lax.ppermute(partial[1], "narrow", [(0, 1), (1, 0)])
            scores = (partial[0] + other) * scale
        else:
            partial = jnp.concatenate([partial[0], partial[1]], axis=1)
            scores = lax.psum_scatter(partial, "narrow", scatter_dimension=1, tiled=True) * scale
        return kernel, factor, scores

    return jax.shard_map(
        on_device,
        mesh=mesh,
        in_specs=(P("wide", "narrow"), P("wide", "narrow"), P("wide")),
        out_specs=(P("wide", "narrow"), P("wide", None), P("wide", "narrow")),
        check_vma=False,
    )
```

time: 167 us -> 159 us (0.952)
  starting transfers between devices: 43.6 us -> 34.5 us
  waiting for transfers between devices: 37.9 us -> 46 us
  Pallas kernels: 67.4 us -> 63.3 us
  local copies, waits for them, and re-layouts: 10.8 us -> 8.09 us
    ppermute x24 -> x22, starting transfers between devices: 42.2 us -> 34 us  [send(): return lax.ppermute(value, 'wide', moves)]
    slice x8 -> x0, local copies, waits for them, and re-layouts: 6.96 us -> none  [the longest x4 3.84 us: on_device(): diag_b = send(across_x[:, half:], swap_y)]
    ppermute x24 -> x22, waiting for transfers between devices: 37.9 us -> 44.8 us  [send(): return lax.ppermute(value, 'wide', moves)]
    pallas_call x5 -> x3, Pallas kernels: 43.6 us -> 38.4 us  [the longest x1 33.4 us: kernel_block(): pl.pallas_call(lambda *refs: kernel_block_body(at, sizes, tile, *refs), i...]
    dynamic_slice x1 -> x4, local copies, waits for them, and re-layouts: 0.01 us -> 2.47 us  [the longest x2 1.69 us: on_device(): lax.dynamic_slice_in_dim(diagonal[r][0], inside, rows_here, axis=1)]
  transfers between devices with their start and end apart: 30 -> 27, of which waited for: 10 -> 12; matrix products, arithmetic and copies ran while one was open for 9% -> 5% of each run, Pallas kernels for 22% -> 19%
where the time goes in v2:
time: 159 us; the launch traced here: 158 us
  Pallas kernels  63.3 us (40%)
  waiting for transfers between devices  46 us (29%)
  starting transfers between devices  34.5 us (22%)
  local copies, waits for them, and re-layouts  8.09 us (5%)
  other arithmetic  5.18 us (3%)
    ppermute x22, waiting for transfers between devices, send(): return lax.ppermute(value, 'wide', moves)  44.8 us
    ppermute x22, starting transfers between devices, send(): return lax.ppermute(value, 'wide', moves)  34 us
    pallas_call x1, Pallas kernels, kernel_block(): pl.pallas_call(lambda *refs: kernel_block_body(at, sizes, tile, *refs), i...  33.4 us
    pallas_call x1, Pallas kernels, second_panel(): pl.pallas_call(second_panel_body, out_shape=(jax.ShapeDtypeStruct((PIVOTS...  10.4 us
    pallas_call x1, Pallas kernels, first_panel(): pl.pallas_call(lambda *refs: first_panel_body(slab, each, *refs), in_spec...  8.35 us
    pallas_call x1, Pallas kernels, early_rows(): pl.pallas_call(body, in_specs=[pl.BlockSpec(memory_space=pltpu.SMEM)] + [...  6.16 us
    pallas_call x2, Pallas kernels, own_rows(): pl.pallas_call(own_rows_body, in_specs=[pl.BlockSpec(memory_space=pltpu.S...  5.04 us
    unnamed x34, local copies, waits for them, and re-layouts  3.28 us
  transfers between devices with their start and end apart: 27, of which 12 were waited for; matrix products, arithmetic and copies ran while one was open for 5% of the time, Pallas kernels for 19%

profile of v2, /device:TPU:0, one launch (start us, length us, event | category | flops | bytes accessed | tf_op | source)
XLA Modules:
  0.0 158.0 jit_solution(18320676852629104499)
XLA Ops:
  0.6 5.1 %collective-permute-start.13 = (bf16[32,8192]{1,0:T(8,128)(2,1)}, bf16[32,8192]{1,0:T(8,128)(2,1)S(1)}, u32[]{:S(2)}, u32[]{:S(2)}) collective-permute-start(bf16[32,8192]{1,0:T(8,128)(2,1)} %refs_10_.1), channel_id=1, source_target_pairs={{0,24},{2,26},{4,28},{6,30},{8,0},{10,2},{12,4},{14,6},{16,8},{18,... | collective-permute-start | bytes 1572872 | tf_op jit(solution)/shard_map/ppermute | solution.py:364
  5.8 1.5 collective-permute-start.7
  8.9 1.6 collective-permute-start
  10.5 2.3 %collective-permute-done = bf16[48,256]{1,0:T(8,128)(2,1)S(1)} collective-permute-done((bf16[48,256]{1,0:T(8,128)(2,1)S(1)}, bf16[48,256]{1,0:T(8,128)(2,1)S(1)}, u32[]{:S(2)}, u32[]{:S(2)}) %collective-permute-start) | collective-permute-done | bytes 24608 | tf_op jit(solution)/shard_map/ppermute | solution.py:364
  13.3 1.5 collective-permute-start.6
  14.8 3.6 %collective-permute-done.13.refs_8_.refs_23_ = bf16[32,8192]{1,0:T(8,128)(2,1)S(1)} collective-permute-done((bf16[32,8192]{1,0:T(8,128)(2,1)}, bf16[32,8192]{1,0:T(8,128)(2,1)S(1)}, u32[]{:S(2)}, u32[]{:S(2)}) %collective-permute-start.13) | collective-permute-done | bytes 524320 | tf_op jit(solution)/shard_map/ppermute | solution.py:364
  18.4 1.5 collective-permute-start.15
  19.9 9.4 %collective-permute-done.9.refs_4_.refs_14_ = bf16[32,8192]{1,0:T(8,128)(2,1)S(1)} collective-permute-done((bf16[32,8192]{1,0:T(8,128)(2,1)}, bf16[32,8192]{1,0:T(8,128)(2,1)S(1)}, u32[]{:S(2)}, u32[]{:S(2)}) %collective-permute-start.9) | collective-permute-done | bytes 524320 | tf_op jit(solution)/shard_map/ppermute | solution.py:364
  29.3 1.6 %collective-permute-start.17 = (bf16[32,8192]{1,0:T(8,128)(2,1)S(1)}, bf16[32,8192]{1,0:T(8,128)(2,1)}, u32[]{:S(2)}, u32[]{:S(2)}) collective-permute-start(bf16[32,8192]{1,0:T(8,128)(2,1)S(1)} %collective-permute-done.9.refs_4_.refs_14_), channel_id=1, source_target_pairs={{0,8},{2,10},{4,12},{6,14},{8,16},{10,18},{12,20},{14,22},{16,24},... | collective-permute-start | bytes 1572872 | tf_op jit(solution)/shard_map/ppermute | solution.py:364
  30.9 1.5 collective-permute-start.10
  33.6 1.5 collective-permute-start.11
  35.1 1.5 collective-permute-start.8
  36.6 7.4 %collective-permute-done.17.refs_0_.refs_18_ = bf16[32,8192]{1,0:T(8,128)(2,1)} collective-permute-done((bf16[32,8192]{1,0:T(8,128)(2,1)S(1)}, bf16[32,8192]{1,0:T(8,128)(2,1)}, u32[]{:S(2)}, u32[]{:S(2)}) %collective-permute-start.17) | collective-permute-done | bytes 524320 | tf_op jit(solution)/shard_map/ppermute | solution.py:364
  44.0 1.5 collective-permute-start.18
  45.8 1.5 collective-permute-start.12
  48.0 9.1 %collective-permute-done.14.refs_9_.refs_24_ = bf16[32,8192]{1,0:T(8,128)(2,1)} collective-permute-done((bf16[32,8192]{1,0:T(8,128)(2,1)S(1)}, bf16[32,8192]{1,0:T(8,128)(2,1)}, u32[]{:S(2)}, u32[]{:S(2)}) %collective-permute-start.14) | collective-permute-done | bytes 524320 | tf_op jit(solution)/shard_map/ppermute | solution.py:364
  58.5 2.1 %collective-permute-start.2 = (bf16[4,48,256]{2,1,0:T(8,128)(2,1)}, bf16[4,48,256]{2,1,0:T(8,128)(2,1)}, u32[]{:S(2)}, u32[]{:S(2)}) collective-permute-start(bf16[4,48,256]{2,1,0:T(8,128)(2,1)} %get-tuple-element.26), channel_id=1, source_target_pairs={{0,8},{2,10},{4,12},{6,14},{8,16},{10,18},{12,20},{14,22},{16,24},... | collective-permute-start | bytes 294920 | tf_op jit(solution)/shard_map/ppermute | solution.py:364
  60.6 7.6 %collective-permute-done.8.refs_3_.refs_13_ = bf16[32,8192]{1,0:T(8,128)(2,1)S(1)} collective-permute-done((bf16[32,8192]{1,0:T(8,128)(2,1)S(1)}, bf16[32,8192]{1,0:T(8,128)(2,1)S(1)}, u32[]{:S(2)}, u32[]{:S(2)}) %collective-permute-start.8) | collective-permute-done | bytes 524320 | tf_op jit(solution)/shard_map/ppermute | solution.py:364
  68.2 2.2 %collective-permute-start.4 = (bf16[4,48,256]{2,1,0:T(8,128)(2,1)}, bf16[4,48,256]{2,1,0:T(8,128)(2,1)}, u32[]{:S(2)}, u32[]{:S(2)}) collective-permute-start(bf16[4,48,256]{2,1,0:T(8,128)(2,1)} %get-tuple-element.26), channel_id=1, source_target_pairs={{0,24},{2,26},{4,28},{6,30},{8,0},{10,2},{12,4},{14,6},{16,8},{18,... | collective-permute-start | bytes 294920 | tf_op jit(solution)/shard_map/ppermute | solution.py:364
  71.2 1.5 collective-permute-start.21
  72.7 2.8 %own_rows.2.refs_0_ = bf16[352,1024]{1,0:T(8,128)(2,1)} custom-call(s32[2]{0:T(128)} %pad_add_fusion.1.home_ref, bf16[32,8192]{1,0:T(8,128)(2,1)} %refs_10_.1, bf16[32,8192]{1,0:T(8,128)(2,1)} %copy-done.7, bf16[32,8192]{1,0:T(8,128)(2,1)} %copy-done.6, bf16[32,8192]{1,0:T(8,128)(2,1)} %copy-done.9, bf16[32,8192]{1,0:T(8,128)(2,1)} %copy-done.5, ...), custom_call_target="tpu_custom_call" | custom-call | tf_op jit(solution)/shard_map/own_rows/pallas_call | solution.py:157
  75.5 1.6 %collective-permute-start.19 = (bf16[32,8192]{1,0:T(8,128)(2,1)}, bf16[32,8192]{1,0:T(8,128)(2,1)S(1)}, u32[]{:S(2)}, u32[]{:S(2)}) collective-permute-start(bf16[32,8192]{1,0:T(8,128)(2,1)} %collective-permute-done.17.refs_0_.refs_18_), channel_id=1, source_target_pairs={{0,4},{2,6},{4,0},{6,2},{8,12},{10,14},{12,8},{14,10},{16,20},{18,... | collective-permute-start | bytes 1572872 | tf_op jit(solution)/shard_map/ppermute | solution.py:364
  77.1 2.3 %collective-permute-done.18.refs_1_.refs_19_ = bf16[32,8192]{1,0:T(8,128)(2,1)S(1)} collective-permute-done((bf16[32,8192]{1,0:T(8,128)(2,1)}, bf16[32,8192]{1,0:T(8,128)(2,1)S(1)}, u32[]{:S(2)}, u32[]{:S(2)}) %collective-permute-start.18) | collective-permute-done | bytes 524320 | tf_op jit(solution)/shard_map/ppermute | solution.py:364
  79.5 1.6 %collective-permute-start.22 = (bf16[32,4096]{1,0:T(8,128)(2,1)S(1)}, bf16[32,4096]{1,0:T(8,128)(2,1)}, u32[]{:S(2)}, u32[]{:S(2)}) collective-permute-start(bf16[32,4096]{1,0:T(8,128)(2,1)S(1)} %get-tuple-element.24), channel_id=1, source_target_pairs={{0,4},{2,6},{4,0},{6,2},{8,12},{10,14},{12,8},{14,10},{16,20},{18,... | collective-permute-start | bytes 786440 | tf_op jit(solution)/shard_map/ppermute | solution.py:364
  82.9 1.5 collective-permute-start.25
  85.3 2.0 %collective-permute-done.19.refs_2_.refs_20_ = bf16[32,8192]{1,0:T(8,128)(2,1)S(1)} collective-permute-done((bf16[32,8192]{1,0:T(8,128)(2,1)}, bf16[32,8192]{1,0:T(8,128)(2,1)S(1)}, u32[]{:S(2)}, u32[]{:S(2)}) %collective-permute-start.19) | collective-permute-done | bytes 524320 | tf_op jit(solution)/shard_map/ppermute | solution.py:364
  88.1 2.3 %own_rows.3.refs_6_ = bf16[96,1024]{1,0:T(8,128)(2,1)} custom-call(s32[2]{0:T(128)} %pad_add_fusion.1.home_ref, bf16[32,8192]{1,0:T(8,128)(2,1)} %collective-permute-done.17.refs_0_.refs_18_, bf16[32,8192]{1,0:T(8,128)(2,1)} %copy-done.1, bf16[32,8192]{1,0:T(8,128)(2,1)} %copy-done.11), custom_call_target="tpu_custom_call" | custom-call | tf_op jit(solution)/shard_map/own_rows/pallas_call | solution.py:157
  90.7 1.5 collective-permute-start.24
  94.5 8.4 %first_panel.1 = (bf16[512,256]{1,0:T(8,128)(2,1)}, f32[128,128]{1,0:T(8,128)}, f32[128,128]{1,0:T(8,128)}, f32[128,128]{1,0:T(8,128)}) custom-call(s32[2]{0:T(128)} %pad_add_fusion.refs_0_, bf16[16,48,256]{2,1,0:T(8,128)(2,1)} %bitcast.25, bf16[16,48,256]{2,1,0:T(8,128)(2,1)} %bitcast.26), custom_call_target="tpu_custom_call" | custom-call | tf_op jit(solution)/shard_map/first_panel/pallas_call | solution.py:98
  102.8 10.4 %second_panel.1 = (f32[256,256]{1,0:T(8,128)}, bf16[3,512,768]{2,1,0:T(8,128)(2,1)}) custom-call(f32[1,1024]{1,0:T(1,128)} %bitcast.31, f32[128,128]{1,0:T(8,128)} %get-tuple-element.12.inv_ref, f32[128,128]{1,0:T(8,128)} %get-tuple-element.13.left_ref, f32[128,128]{1,0:T(8,128)} %get-tuple-element.14.rest_ref, bf16[512,256]{1,0:T(8,128)(2,1)} %get-tuple-element.15.fp_ref), custom_call_target="tpu_custom_call" | custom-call | tf_op jit(solution)/shard_map/second_panel/pallas_call | solution.py:129
  114.1 6.2 %early_rows.1.refs_3_ = f32[1024,768]{1,0:T(8,128)} custom-call(s32[2]{0:T(128)} %pad_add_fusion.1.home_ref, bf16[3,512,768]{2,1,0:T(8,128)(2,1)} %get-tuple-element.17.factors_ref.refs_4_, bf16[352,1024]{1,0:T(8,128)(2,1)} %own_rows.2.refs_0_, bf16[352,1024]{1,0:T(8,128)(2,1)} %copy-done.3), custom_call_target="tpu_custom_call" | custom-call | tf_op jit(solution)/shard_map/early_rows/pallas_call | solution.py:180
  121.1 33.4 %kernel_block.1 = (f32[1024,8192]{1,0:T(8,128)}, f32[1024,256]{1,0:T(8,128)}, f32[2,64,256]{2,1,0:T(8,128)}) custom-call(s32[6]{0:T(128)} %stack.80.refs_0_, f32[1,1024]{1,0:T(1,128)} %bitcast.32, f32[256,256]{1,0:T(8,128)} %get-tuple-element.16.refs_2_, f32[1024,768]{1,0:T(8,128)} %early_rows.1.refs_3_, ...), custom_call_target="tpu_custom_call" | custom-call | flops 17179869184 | bytes 41943040 | tf_op jit(solution)/shard_map/kernel_block/pallas_call | solution.py:308
  (82 shorter events, 17.8 us)
Async XLA Ops:
  0.6 17.8 %collective-permute-start.13 = (bf16[32,8192]{1,0:T(8,128)(2,1)}, bf16[32,8192]{1,0:T(8,128)(2,1)S(1)}, u32[]{:S(2)}, u32[]{:S(2)}) collective-permute-start(bf16[32,8192]{1,0:T(8,128)(2,1)} %refs_10_.1), channel_id=1, source_target_pairs={{0,24},{2,26},{4,28},{6,30},{8,0},{10,2},{12,4},{14,6},{16,8},{18,... | collective-permute-start | bytes 1572872 | tf_op jit(solution)/shard_map/ppermute | solution.py:364
  5.8 23.5 %collective-permute-start.9 = (bf16[32,8192]{1,0:T(8,128)(2,1)}, bf16[32,8192]{1,0:T(8,128)(2,1)S(1)}, u32[]{:S(2)}, u32[]{:S(2)}) collective-permute-start(bf16[32,8192]{1,0:T(8,128)(2,1)} %refs_10_.1), channel_id=1, source_target_pairs={{0,8},{2,10},{4,12},{6,14},{8,16},{10,18},{12,20},{14,22},{16,24},... | collective-permute-start | bytes 1572872 | tf_op jit(solution)/shard_map/ppermute | solution.py:364
  5.8 26.7 %collective-permute-start.7 = (bf16[32,8192]{1,0:T(8,128)(2,1)}, bf16[32,8192]{1,0:T(8,128)(2,1)S(1)}, u32[]{:S(2)}, u32[]{:S(2)}) collective-permute-start(bf16[32,8192]{1,0:T(8,128)(2,1)} %refs_10_.1), channel_id=1, source_target_pairs={{0,4},{2,6},{4,0},{6,2},{8,12},{10,14},{12,8},{14,10},{16,20},{18,... | collective-permute-start | bytes 1572872 | tf_op jit(solution)/shard_map/ppermute | solution.py:364
  8.9 3.9 %collective-permute-start = (bf16[48,256]{1,0:T(8,128)(2,1)S(1)}, bf16[48,256]{1,0:T(8,128)(2,1)S(1)}, u32[]{:S(2)}, u32[]{:S(2)}) collective-permute-start(bf16[48,256]{1,0:T(8,128)(2,1)S(1)} %concatenate.10), channel_id=1, source_target_pairs={{0,2},{2,0},{4,6},{6,4},{8,10},{10,8},{12,14},{14,12},{16,18},{18,... | collective-permute-start | bytes 73736 | tf_op jit(solution)/shard_map/ppermute | solution.py:364
  12.8 18.1 %collective-permute-start.1 = (bf16[2,48,256]{2,1,0:T(8,128)(2,1)S(1)}, bf16[2,48,256]{2,1,0:T(8,128)(2,1)S(1)}, u32[]{:S(2)}, u32[]{:S(2)}) collective-permute-start(bf16[2,48,256]{2,1,0:T(8,128)(2,1)S(1)} %pad_maximum_fusion.3), channel_id=1, source_target_pairs={{0,4},{2,6},{4,0},{6,2},{8,12},{10,14},{12,8},{14,10},{16,20},{18,... | collective-permute-start | bytes 147464 | tf_op jit(solution)/shard_map/ppermute | solution.py:364
  13.3 20.3 %collective-permute-start.6 = (bf16[32,8192]{1,0:T(8,128)(2,1)}, bf16[32,8192]{1,0:T(8,128)(2,1)S(1)}, u32[]{:S(2)}, u32[]{:S(2)}) collective-permute-start(bf16[32,8192]{1,0:T(8,128)(2,1)} %refs_10_.1), channel_id=1, source_target_pairs={{0,2},{2,0},{4,6},{6,4},{8,10},{10,8},{12,14},{14,12},{16,18},{18,... | collective-permute-start | bytes 1572872 | tf_op jit(solution)/shard_map/ppermute | solution.py:364
  18.4 54.3 %copy-start.4 = (bf16[32,8192]{1,0:T(8,128)(2,1)}, bf16[32,8192]{1,0:T(8,128)(2,1)S(1)}, u32[]{:S(2)}) copy-start(bf16[32,8192]{1,0:T(8,128)(2,1)S(1)} %collective-permute-done.13.refs_8_.refs_23_) | copy-start | bytes 1572868
  18.4 16.7 %collective-permute-start.15 = (bf16[32,8192]{1,0:T(8,128)(2,1)S(1)}, bf16[32,8192]{1,0:T(8,128)(2,1)S(1)}, u32[]{:S(2)}, u32[]{:S(2)}) collective-permute-start(bf16[32,8192]{1,0:T(8,128)(2,1)S(1)} %collective-permute-done.13.refs_8_.refs_23_), channel_id=1, source_target_pairs={{0,4},{2,6},{4,0},{6,2},{8,12},{10,14},{12,8},{14,10},{16,20},{18,... | collective-permute-start | bytes 1572872 | tf_op jit(solution)/shard_map/ppermute | solution.py:364
  29.3 43.4 %copy-start.5 = (bf16[32,8192]{1,0:T(8,128)(2,1)}, bf16[32,8192]{1,0:T(8,128)(2,1)S(1)}, u32[]{:S(2)}) copy-start(bf16[32,8192]{1,0:T(8,128)(2,1)S(1)} %collective-permute-done.9.refs_4_.refs_14_) | copy-start | bytes 1572868
  29.3 14.7 %collective-permute-start.17 = (bf16[32,8192]{1,0:T(8,128)(2,1)S(1)}, bf16[32,8192]{1,0:T(8,128)(2,1)}, u32[]{:S(2)}, u32[]{:S(2)}) collective-permute-start(bf16[32,8192]{1,0:T(8,128)(2,1)S(1)} %collective-permute-done.9.refs_4_.refs_14_), channel_id=1, source_target_pairs={{0,8},{2,10},{4,12},{6,14},{8,16},{10,18},{12,20},{14,22},{16,24},... | collective-permute-start | bytes 1572872 | tf_op jit(solution)/shard_map/ppermute | solution.py:364
  30.9 14.9 %collective-permute-start.10 = (bf16[32,8192]{1,0:T(8,128)(2,1)S(1)}, bf16[32,8192]{1,0:T(8,128)(2,1)}, u32[]{:S(2)}, u32[]{:S(2)}) collective-permute-start(bf16[32,8192]{1,0:T(8,128)(2,1)S(1)} %collective-permute-done.9.refs_4_.refs_14_), channel_id=1, source_target_pairs={{0,2},{2,0},{4,6},{6,4},{8,10},{10,8},{12,14},{14,12},{16,18},{18,... | collective-permute-start | bytes 1572872 | tf_op jit(solution)/shard_map/ppermute | solution.py:364
  32.4 40.3 %copy-start.6 = (bf16[32,8192]{1,0:T(8,128)(2,1)}, bf16[32,8192]{1,0:T(8,128)(2,1)S(1)}, u32[]{:S(2)}) copy-start(bf16[32,8192]{1,0:T(8,128)(2,1)S(1)} %collective-permute-done.7.refs_2_.refs_12_) | copy-start | bytes 1572868
  32.4 24.6 %collective-permute-start.14 = (bf16[32,8192]{1,0:T(8,128)(2,1)S(1)}, bf16[32,8192]{1,0:T(8,128)(2,1)}, u32[]{:S(2)}, u32[]{:S(2)}) collective-permute-start(bf16[32,8192]{1,0:T(8,128)(2,1)S(1)} %collective-permute-done.13.refs_8_.refs_23_), channel_id=1, source_target_pairs={{0,2},{2,0},{4,6},{6,4},{8,10},{10,8},{12,14},{14,12},{16,18},{18,... | collective-permute-start | bytes 1572872 | tf_op jit(solution)/shard_map/ppermute | solution.py:364
  33.6 39.1 %copy-start.7 = (bf16[32,8192]{1,0:T(8,128)(2,1)}, bf16[32,8192]{1,0:T(8,128)(2,1)S(1)}, u32[]{:S(2)}) copy-start(bf16[32,8192]{1,0:T(8,128)(2,1)S(1)} %collective-permute-done.6.refs_1_.refs_11_) | copy-start | bytes 1572868
  33.6 24.9 %collective-permute-start.11 = (bf16[32,8192]{1,0:T(8,128)(2,1)S(1)}, bf16[32,8192]{1,0:T(8,128)(2,1)S(1)}, u32[]{:S(2)}, u32[]{:S(2)}) collective-permute-start(bf16[32,8192]{1,0:T(8,128)(2,1)S(1)} %collective-permute-done.9.refs_4_.refs_14_), channel_id=1, source_target_pairs={{0,4},{2,6},{4,0},{6,2},{8,12},{10,14},{12,8},{14,10},{16,20},{18,... | collective-permute-start | bytes 1572872 | tf_op jit(solution)/shard_map/ppermute | solution.py:364
  35.1 37.6 %copy-start = (bf16[32,8192]{1,0:T(8,128)(2,1)}, bf16[32,8192]{1,0:T(8,128)(2,1)S(1)}, u32[]{:S(2)}) copy-start(bf16[32,8192]{1,0:T(8,128)(2,1)S(1)} %collective-permute-done.15.refs_10_.refs_25_) | copy-start | bytes 1572868
  35.1 33.1 %collective-permute-start.8 = (bf16[32,8192]{1,0:T(8,128)(2,1)S(1)}, bf16[32,8192]{1,0:T(8,128)(2,1)S(1)}, u32[]{:S(2)}, u32[]{:S(2)}) collective-permute-start(bf16[32,8192]{1,0:T(8,128)(2,1)S(1)} %collective-permute-done.7.refs_2_.refs_12_), channel_id=1, source_target_pairs={{0,2},{2,0},{4,6},{6,4},{8,10},{10,8},{12,14},{14,12},{16,18},{18,... | collective-permute-start | bytes 1572872 | tf_op jit(solution)/shard_map/ppermute | solution.py:364
  44.0 35.4 %collective-permute-start.18 = (bf16[32,8192]{1,0:T(8,128)(2,1)}, bf16[32,8192]{1,0:T(8,128)(2,1)S(1)}, u32[]{:S(2)}, u32[]{:S(2)}) collective-permute-start(bf16[32,8192]{1,0:T(8,128)(2,1)} %collective-permute-done.17.refs_0_.refs_18_), channel_id=1, source_target_pairs={{0,2},{2,0},{4,6},{6,4},{8,10},{10,8},{12,14},{14,12},{16,18},{18,... | collective-permute-start | bytes 1572872 | tf_op jit(solution)/shard_map/ppermute | solution.py:364
  45.8 24.6 %collective-permute-start.12 = (bf16[32,8192]{1,0:T(8,128)(2,1)}, bf16[32,8192]{1,0:T(8,128)(2,1)S(1)}, u32[]{:S(2)}, u32[]{:S(2)}) collective-permute-start(bf16[32,8192]{1,0:T(8,128)(2,1)} %collective-permute-done.10.refs_5_.refs_15_), channel_id=1, source_target_pairs={{0,4},{2,6},{4,0},{6,2},{8,12},{10,14},{12,8},{14,10},{16,20},{18,... | collective-permute-start | bytes 1572872 | tf_op jit(solution)/shard_map/ppermute | solution.py:364
  57.1 18.4 %collective-permute-start.3 = (bf16[4,48,256]{2,1,0:T(8,128)(2,1)}, bf16[4,48,256]{2,1,0:T(8,128)(2,1)}, u32[]{:S(2)}, u32[]{:S(2)}) collective-permute-start(bf16[4,48,256]{2,1,0:T(8,128)(2,1)} %get-tuple-element.26), channel_id=1, source_target_pairs={{0,16},{2,18},{4,20},{6,22},{8,24},{10,26},{12,28},{14,30},{16,0},... | collective-permute-start | bytes 294920 | tf_op jit(solution)/shard_map/ppermute | solution.py:364
  58.5 21.0 %collective-permute-start.2 = (bf16[4,48,256]{2,1,0:T(8,128)(2,1)}, bf16[4,48,256]{2,1,0:T(8,128)(2,1)}, u32[]{:S(2)}, u32[]{:S(2)}) collective-permute-start(bf16[4,48,256]{2,1,0:T(8,128)(2,1)} %get-tuple-element.26), channel_id=1, source_target_pairs={{0,8},{2,10},{4,12},{6,14},{8,16},{10,18},{12,20},{14,22},{16,24},... | collective-permute-start | bytes 294920 | tf_op jit(solution)/shard_map/ppermute | solution.py:364
  68.2 12.9 %collective-permute-start.4 = (bf16[4,48,256]{2,1,0:T(8,128)(2,1)}, bf16[4,48,256]{2,1,0:T(8,128)(2,1)}, u32[]{:S(2)}, u32[]{:S(2)}) collective-permute-start(bf16[4,48,256]{2,1,0:T(8,128)(2,1)} %get-tuple-element.26), channel_id=1, source_target_pairs={{0,24},{2,26},{4,28},{6,30},{8,0},{10,2},{12,4},{14,6},{16,8},{18,... | collective-permute-start | bytes 294920 | tf_op jit(solution)/shard_map/ppermute | solution.py:364
  71.2 11.7 %collective-permute-start.21 = (bf16[32,4096]{1,0:T(8,128)(2,1)}, bf16[32,4096]{1,0:T(8,128)(2,1)}, u32[]{:S(2)}, u32[]{:S(2)}) collective-permute-start(bf16[32,4096]{1,0:T(8,128)(2,1)} %get-tuple-element.22), channel_id=1, source_target_pairs={{0,2},{2,0},{4,6},{6,4},{8,10},{10,8},{12,14},{14,12},{16,18},{18,... | collective-permute-start | bytes 786440 | tf_op jit(solution)/shard_map/ppermute | solution.py:364
  75.5 11.8 %collective-permute-start.19 = (bf16[32,8192]{1,0:T(8,128)(2,1)}, bf16[32,8192]{1,0:T(8,128)(2,1)S(1)}, u32[]{:S(2)}, u32[]{:S(2)}) collective-permute-start(bf16[32,8192]{1,0:T(8,128)(2,1)} %collective-permute-done.17.refs_0_.refs_18_), channel_id=1, source_target_pairs={{0,4},{2,6},{4,0},{6,2},{8,12},{10,14},{12,8},{14,10},{16,20},{18,... | collective-permute-start | bytes 1572872 | tf_op jit(solution)/shard_map/ppermute | solution.py:364
  79.4 33.8 %collective-permute-start.16 = (bf16[352,1024]{1,0:T(8,128)(2,1)}, bf16[352,1024]{1,0:T(8,128)(2,1)S(1)}, u32[]{:S(2)}, u32[]{:S(2)}) collective-permute-start(bf16[352,1024]{1,0:T(8,128)(2,1)} %own_rows.2.refs_0_), channel_id=1, source_target_pairs={{0,1},{1,0},{2,3},{3,2},{4,5},{5,4},{6,7},{7,6},{8,9},{9,8},{10,11... | collective-permute-start | bytes 2162696 | tf_op jit(solution)/shard_map/ppermute | solution.py:368
  79.5 11.2 %collective-permute-start.22 = (bf16[32,4096]{1,0:T(8,128)(2,1)S(1)}, bf16[32,4096]{1,0:T(8,128)(2,1)}, u32[]{:S(2)}, u32[]{:S(2)}) collective-permute-start(bf16[32,4096]{1,0:T(8,128)(2,1)S(1)} %get-tuple-element.24), channel_id=1, source_target_pairs={{0,4},{2,6},{4,0},{6,2},{8,12},{10,14},{12,8},{14,10},{16,20},{18,... | collective-permute-start | bytes 786440 | tf_op jit(solution)/shard_map/ppermute | solution.py:364
  82.1 10.9 %collective-permute-start.5 = (bf16[4,4,48,256]{3,2,1,0:T(8,128)(2,1)S(1)}, bf16[4,4,48,256]{3,2,1,0:T(8,128)(2,1)S(1)}, u32[]{:S(2)}, u32[]{:S(2)}) collective-permute-start(bf16[4,4,48,256]{3,2,1,0:T(8,128)(2,1)S(1)} %pad_maximum_fusion), channel_id=1, source_target_pairs={{0,1},{1,0},{2,3},{3,2},{4,5},{5,4},{6,7},{7,6},{8,9},{9,8},{10,11... | collective-permute-start | bytes 1179656 | tf_op jit(solution)/shard_map/ppermute | solution.py:368
  82.9 37.3 %collective-permute-start.25 = (bf16[32,4096]{1,0:T(8,128)(2,1)S(1)}, bf16[32,4096]{1,0:T(8,128)(2,1)}, u32[]{:S(2)}, u32[]{:S(2)}) collective-permute-start(bf16[32,4096]{1,0:T(8,128)(2,1)S(1)} %get-tuple-element.21), channel_id=1, source_target_pairs={{0,2},{2,0},{4,6},{6,4},{8,10},{10,8},{12,14},{14,12},{16,18},{18,... | collective-permute-start | bytes 786440 | tf_op jit(solution)/shard_map/ppermute | solution.py:364
  90.3 29.9 %collective-permute-start.20 = (bf16[96,1024]{1,0:T(8,128)(2,1)}, bf16[96,1024]{1,0:T(8,128)(2,1)S(1)}, u32[]{:S(2)}, u32[]{:S(2)}) collective-permute-start(bf16[96,1024]{1,0:T(8,128)(2,1)} %own_rows.3.refs_6_), channel_id=1, source_target_pairs={{0,1},{1,0},{2,3},{3,2},{4,5},{5,4},{6,7},{7,6},{8,9},{9,8},{10,11... | collective-permute-start | bytes 589832 | tf_op jit(solution)/shard_map/ppermute | solution.py:368
  90.7 29.6 %collective-permute-start.24 = (bf16[32,4096]{1,0:T(8,128)(2,1)S(1)}, bf16[32,4096]{1,0:T(8,128)(2,1)S(1)}, u32[]{:S(2)}, u32[]{:S(2)}) collective-permute-start(bf16[32,4096]{1,0:T(8,128)(2,1)S(1)} %get-tuple-element.23), channel_id=1, source_target_pairs={{0,4},{2,6},{4,0},{6,2},{8,12},{10,14},{12,8},{14,10},{16,20},{18,... | collective-permute-start | bytes 786440 | tf_op jit(solution)/shard_map/ppermute | solution.py:364
  93.1 27.2 %collective-permute-start.23 = (bf16[64,1024]{1,0:T(8,128)(2,1)S(1)}, bf16[64,1024]{1,0:T(8,128)(2,1)S(1)}, u32[]{:S(2)}, u32[]{:S(2)}) collective-permute-start(bf16[64,1024]{1,0:T(8,128)(2,1)S(1)} %pad_maximum_fusion.1.refs_8_), channel_id=1, source_target_pairs={{0,1},{1,0},{2,3},{3,2},{4,5},{5,4},{6,7},{7,6},{8,9},{9,8},{10,11... | collective-permute-start | bytes 393224 | tf_op jit(solution)/shard_map/ppermute | solution.py:368
  155.3 1.3 collective-permute-start.26
  (12 other events, 65.4 us)
